TPU v7x, 128 devices: a whole 4x4x4 slice. The times are simulated.
128 devices in a mesh: row: 16 (over z, y_hi, core), col: 8 (over y_lo, x).
Axes of the slice: x: 4, y: 4 (y_hi: 2, y_lo: 2; y = y_hi * 2 + y_lo), z: 4, core: 2. Of those that a mesh axis runs over, the one named last changes fastest.
Arguments:
- reflectivity: float32 [128, 512, 2048], P(('row', 'col')), may hold values from 0 to 40
- scan_hour: int32 [128], replicated, may hold values from 0 to 11, as said below
- basin_ids: int32 [512, 16], P('row', 'col'), may hold values from 0 to 1023, as said below
Outputs:
- hourly_depth: float32 [12, 512, 2048], P(None, 'row', 'col')
- basin_depth: float32 [1024, 12], P(('row', 'col'))
Inputs may be any that keep to these rules, and one draw needn't show every extreme that they name: scan_hour starts at 0, never falls, rises by at most one from one scan to the next, and every hour has 1 to 12 scans. `basin_ids`: every basin is named by at least one segment, and all segments of a basin lie in one aligned block of 8 grid rows.
All inputs are finite; a program needn't handle non-finite values.
Results may differ from a plain program's by a relative error of at most 0.00021.
Values sent between devices are 32-bit elements; how exact they have to be, the bound alone decides.
A program may use at most 64 MiB of HBM per device.

v0:
```python
import math

import jax
import jax.numpy as jnp
from jax import lax
from jax.sharding import PartitionSpec as P

SEG = 128
BASIN_ROWS = 8


slope_db = math.log(10.0) / 16.0
offset_zr = math.log(200.0) / 1.6


def rain_depth(reflect):
    return jnp.exp(reflect * slope_db - offset_zr) / 12.0


def body(reflectivity, scan_hour, basin_ids):
    row_devices = lax.axis_size("row")
    col_devices = lax.axis_size("col")
    scan_block, grid_height, grid_width = reflectivity.shape
    tile_rows = grid_height // row_devices
    tile_cols = grid_width // col_devices
    blocks = reflectivity.reshape(scan_block, row_devices, tile_rows, col_devices, tile_cols)
    blocks = blocks.transpose(0, 1, 3, 2, 4).reshape(
        scan_block, row_devices * col_devices, tile_rows, tile_cols
    )
    arrived = lax.all_to_all(blocks, ("row", "col"), split_axis=1, concat_axis=0, tiled=True)
    pixels = arrived.reshape(-1, tile_rows * tile_cols)
    pixels = rain_depth(pixels)
    hour_count = (scan_hour.shape[0] + 10) // 12 + 1
    selector = (scan_hour[None, :] == jnp.arange(hour_count, dtype=jnp.int32)[:, None]).astype(
        jnp.float32
    )
    hourly = jnp.dot(
        selector, pixels, precision=lax.Precision.HIGHEST, preferred_element_type=jnp.float32
    )
    segment = (
        hourly.reshape(hour_count, tile_rows, tile_cols // SEG, SEG)
        .sum(axis=3)
        .reshape(hour_count, -1)
    )
    basin_list = basin_ids.reshape(-1)
    basin_count = grid_height * grid_width // (SEG * BASIN_ROWS)
    members = (basin_list[:, None] == jnp.arange(basin_count, dtype=jnp.int32)[None, :]).astype(
        jnp.float32
    )
    partial_value = jnp.dot(
        members.T, segment.T, precision=lax.Precision.HIGHEST, preferred_element_type=jnp.float32
    )
    counts = jnp.sum(members, axis=0) * float(SEG)
    totals, basin_pixels = (
        lax.psum_scatter(partial_value, ("row", "col"), scatter_dimension=0, tiled=True),
        lax.psum_scatter(counts, ("row", "col"), scatter_dimension=0, tiled=True),
    )
    return (hourly.reshape(hour_count, tile_rows, tile_cols), totals / basin_pixels[:, None])


def solution(mesh):
    placed = (P(("row", "col"), None, None), P(), P("row", "col"))
    return jax.shard_map(
        body,
        mesh=mesh,
        in_specs=placed,
        out_specs=(P(None, "row", "col"), P(("row", "col"), None)),
        check_vma=False,
    )
```

profile of v0, /device:TPU:1, one launch (start us, length us, event | category | flops | bytes accessed | tf_op | source)
XLA Modules:
  0.0 150.8 jit_solution(14218442369604628147)
XLA Ops:
  0.6 4.1 %copy.17 = f32[64,8,8,256]{3,2,1,0:T(8,128)S(1)} copy(f32[64,8,8,256]{3,1,2,0:T(8,128)} %bitcast.24) | data formatting | bytes 8388608
  4.8 3.3 %copy.13 = f32[1,16,8,32,256]{4,3,2,1,0:T(8,128)} copy(f32[1,16,8,32,256]{4,2,3,1,0:T(8,128)S(1)} %bitcast.22) | data formatting | bytes 8388608 | tf_op jit(solution)/shard_map/transpose | solution.py:27
  8.1 0.0 copy-start
  8.1 12.0 %all-to-all-start = ((f32[1,128,32,256]{3,2,0,1:T(8,128)}), f32[1,128,32,256]{3,2,0,1:T(8,128)}, u32[]{:S(2)}, u32[]{:S(2)}) async-start(f32[1,128,32,256]{3,2,0,1:T(8,128)} %bitcast.19), calls=%async_computation | async-start | bytes 8388608 | tf_op jit(solution)/shard_map/all_to_all | solution.py:30
  20.0 0.0 copy-done
  20.0 0.1 copy.15
  20.1 0.1 eq.31
  20.2 0.1 convert_reduce_fusion
  20.4 52.0 %all-to-all-done = f32[1,128,32,256]{3,2,0,1:T(8,128)} async-done(((f32[1,128,32,256]{3,2,0,1:T(8,128)}), f32[1,128,32,256]{3,2,0,1:T(8,128)}, u32[]{:S(2)}, u32[]{:S(2)}) %all-to-all-start) | async-done | bytes 4194336 | tf_op jit(solution)/shard_map/all_to_all | solution.py:30
  72.3 3.1 %exponential_multiply_fusion = f32[1,128,32,256]{3,2,0,1:T(8,128)S(1)} fusion(f32[1,128,32,256]{3,2,0,1:T(8,128)} %all-to-all-done), kind=kLoop, calls=%fused_computation | loop fusion | flops 3145728 | bytes 8388608 | tf_op jit(solution)/shard_map/div | solution.py:17
  75.4 0.0 copy-start.1
  75.4 3.3 %copy.18 = f32[16,8,32,256]{3,1,2,0:T(8,128)S(1)} copy(f32[16,8,32,256]{3,2,1,0:T(8,128)S(1)} %bitcast.20) | data formatting | bytes 8388608
  78.7 0.0 copy-done.1
  78.8 1.5 fusion.2
  80.2 0.3 reshape.37
  80.6 0.5 reduce_sum.18
  81.0 0.3 copy.16
  81.4 0.7 fusion
  82.0 0.2 copy.19
  82.2 0.8 slice
  83.0 67.1 %all-reduce.2 = (f32[1024,12]{1,0:T(8,128)S(1)}, f32[1024]{0:T(1024)S(1)}) all-reduce(f32[1024,12]{1,0:T(8,128)S(1)} %fusion, f32[1024]{0:T(1024)S(1)} %broadcast_multiply_fusion), channel_id=2, replica_groups=mesh['row'=16,'col'=8] {'row','col'}, use_global_device_ids=true, to_apply=%region_1.0.clone | all-reduce | flops 13312 | bytes 106496
  150.1 0.1 dynamic-slice.1
  150.2 0.7 dynamic-slice_divide_fusion
  (1 shorter events, 0.0 us)
Async XLA Ops:
  8.1 12.0 %copy-start = (s32[32,2]{0,1:T(2,128)S(1)}, s32[32,2]{0,1:T(2,128)}, u32[]{:S(2)}) copy-start(s32[32,2]{0,1:T(2,128)} %param.5) | copy-start | bytes 772
  8.1 64.3 %all-to-all-start = ((f32[1,128,32,256]{3,2,0,1:T(8,128)}), f32[1,128,32,256]{3,2,0,1:T(8,128)}, u32[]{:S(2)}, u32[]{:S(2)}) async-start(f32[1,128,32,256]{3,2,0,1:T(8,128)} %bitcast.19), calls=%async_computation | async-start | bytes 8388608 | tf_op jit(solution)/shard_map/all_to_all | solution.py:30
  75.4 3.3 %copy-start.1 = (s32[128]{0:T(128)S(1)}, s32[128]{0:T(128)}, u32[]{:S(2)}) copy-start(s32[128]{0:T(128)} %param.4) | copy-start | bytes 1540
where the time goes:
time: 151 us
  blocking collectives  67.1 us (44%)
  waiting for transfers between devices  52 us (34%)
  local copies, waits for them, and re-layouts  12.6 us (8%)
  starting transfers between devices  12 us (8%)
  other arithmetic  4.35 us (3%)
  matrix products  2.14 us (1%)
    unnamed x1, blocking collectives  67.1 us
    all_to_all x1, waiting for transfers between devices, body(): lax.all_to_all(blocks, ('row', 'col'), split_axis=1, concat_axis=0, tiled...  52 us
    all_to_all x1, starting transfers between devices, body(): lax.all_to_all(blocks, ('row', 'col'), split_axis=1, concat_axis=0, tiled...  12 us
    unnamed x9, local copies, waits for them, and re-layouts  7.79 us
    transpose x1, local copies, waits for them, and re-layouts, body(): blocks.transpose(0, 1, 3, 2, 4)  3.28 us
    div x1, other arithmetic, rain_depth(): return jnp.exp(reflect * slope_db - offset_zr) / 12.0  3.1 us
  transfers between devices with their start and end apart: 1, of which 1 were waited for; matrix products, arithmetic and copies ran while one was open for 0% of the time, Pallas kernels for 0%

commit v1 on v0

v1 whole, which is shorter than its diff:
```python
import math

import jax
import jax.numpy as jnp
from jax import lax
from jax.experimental import pallas as pl
from jax.experimental.pallas import tpu as pltpu
from jax.sharding import PartitionSpec as P

MESH = pl.DeviceIdType.MESH
SEG = 128
HOURS = 12
CHUNKS = 4
SLOTS = (4, 5)
LOW = 11
LOG2E = 1.0 / math.log(2.0)
SCALE = math.log(10.0) / 16.0 * LOG2E
SHIFT = (math.log(200.0) / 1.6 + math.log(12.0)) * LOG2E


def rain_depth(reflect):
    return jnp.exp2(reflect * SCALE - SHIFT)


def flip(value, mask):
    if mask == 0:
        return value
    if mask == 1:
        return value + 1 - 2 * (value % 2)
    if mask == 2:
        return (value + 2) % 4
    return 3 - value


def masks(parity):
    return (1, 3) if parity == 0 else (3, 1)


def device(x, y, z, c):
    return (z * 4 + (y // 2) * 2 + c, (y % 2) * 4 + x)


def kernel(
    refl, hours, ids, out, depth,
    src, got1, own_slots0, own_slots1, own_slots2, own_slots3, got2a, got2b, got2c, got2d,
    part, part_got, part_sum, part_last,
    load_sem, send1, recv1, send2, recv2, bsend1, brecv1, bsend2, brecv2,
):
    slots_of = (own_slots0, own_slots1, own_slots2, own_slots3)
    got2_of = (got2a, got2b, got2c, got2d)
    row, col = lax.axis_index("row"), lax.axis_index("col")
    z, c = row // 4, row % 2
    y, x = ((row // 2) % 2) * 2 + col // 4, col % 4

    for j in range(CHUNKS):
        m1, m2 = masks(j % 2)
        for ry1 in range(2):
            for ry2 in range(2):
                dy = flip(y, (m1 * ry1) ^ (m2 * ry2))
                for rx1 in range(2):
                    for rx2 in range(2):
                        dx = flip(x, (m1 * rx1) ^ (m2 * rx2))
                        lanes = pl.ds(pl.multiple_of(((dy % 2) * 4 + dx) * 256, 256), 256)
                        pltpu.make_async_copy(
                            refl.at[:, dy // 2, :, j, :, lanes],
                            src.at[j, ry1, rx1, pl.ds((ry2 * 2 + rx2) * 4, 4)],
                            load_sem.at[j],
                        ).start()

    barrier = pltpu.get_barrier_semaphore()
    peers = []
    for my in (0, 1, 3):
        for mx in (0, 1, 3):
            for dz in range(4):
                for dc in range(2):
                    quad_even = mx in (0, 1) and my in (0, 1)
                    quad_odd = mx in (0, 3) and my in (0, 3)
                    if not (quad_even or quad_odd) or (dc and dz):
                        continue
                    if mx == 0 and my == 0 and dz == 0 and dc == 0:
                        continue
                    peers.append((mx, my, dz, dc))
    for mx, my, dz, dc in peers:
        core = 1 - c if dc else c
        pl.semaphore_signal(
            barrier, inc=1, device_id=device(flip(x, mx), flip(y, my), (z + dz) % 4, core), device_id_type=MESH
        )

    for j in range(CHUNKS):
        empty = jnp.zeros((8, 256), jnp.float32)
        buf, slots = got2_of[j], SLOTS[j % 2]

        @pl.loop(0, 16)
        def _(s):
            for k in range(HOURS + LOW):
                if not LOW <= k < LOW + slots:
                    buf[s, k] = empty

    pl.semaphore_wait(barrier, len(peers))

    def copy1(j, ry1, rx1, tc, sc):
        m1, _ = masks(j % 2)
        return pltpu.make_async_remote_copy(
            src_ref=src.at[j, ry1, rx1, :, tc],
            dst_ref=got1.at[j, ry1, rx1, sc],
            send_sem=send1.at[j, (ry1 * 2 + rx1) * 2 + tc],
            recv_sem=recv1.at[j, (ry1 * 2 + rx1) * 2 + sc],
            device_id=device(flip(x, m1 * rx1), flip(y, m1 * ry1), z, tc),
            device_id_type=MESH,
        )

    quads = [(0, 1), (1, 0), (1, 1)]

    def step1_copies(j, mine):
        found = []
        for ry1, rx1 in quads:
            for core in range(2):
                found.append(copy1(j, ry1, rx1, core, c) if mine else copy1(j, ry1, rx1, c, core))
        found.append(copy1(j, 0, 0, 1 - c, c) if mine else copy1(j, 0, 0, c, 1 - c))
        return found

    for j in range(CHUNKS):
        pltpu.make_async_copy(src.at[j], src.at[j], load_sem.at[j]).wait()
        for copy in step1_copies(j, True):
            copy.start()

    def base_scan(j, yy, zz):
        return zz * 32 + (yy // 2) * 16 if j % 2 == 0 else zz * 32

    def reduce1(j):
        m1, _ = masks(j % 2)
        slots = SLOTS[j % 2]
        first = hours[base_scan(j, y, z)]
        weights = []
        for ry1 in range(2):
            for rx1 in range(2):
                for core in range(2):
                    yy, xx = flip(y, m1 * ry1), flip(x, m1 * rx1)
                    cc = core if ry1 + rx1 else (c if core == 0 else 1 - c)
                    hour = hours[z * 32 + (yy // 2) * 16 + cc * 8 + (yy % 2) * 4 + xx]
                    weights.append([jnp.where(hour - first == k, 1.0, 0.0).astype(jnp.float32) for k in range(slots)])

        @pl.loop(0, 16)
        def _(t):
            total = [None] * slots
            n = 0
            for ry1 in range(2):
                for rx1 in range(2):
                    for core in range(2):
                        if ry1 + rx1:
                            raw = got1[j, ry1, rx1, core, t]
                        elif core == 0:
                            raw = src[j, 0, 0, t, c]
                        else:
                            raw = got1[j, 0, 0, 1 - c, t]
                        value = rain_depth(raw)
                        for k in range(slots):
                            term = value * weights[n][k]
                            total[k] = term if total[k] is None else total[k] + term
                        n += 1
            for k in range(slots):
                slots_of[j][t, k] = total[k]

    def copy2(j, q, dz, mine):
        _, m2 = masks(j % 2)
        ry2, rx2 = q // 2, q % 2
        slots = SLOTS[j % 2]
        target_z = (z + dz) % 4
        return pltpu.make_async_remote_copy(
            src_ref=slots_of[j].at[q * 4 + target_z],
            dst_ref=got2_of[j].at[q * 4 + dz, pl.ds(LOW, slots)],
            send_sem=send2.at[j, q * 4 + dz],
            recv_sem=recv2.at[j, q * 4 + dz],
            device_id=device(flip(x, m2 * rx2), flip(y, m2 * ry2), target_z, c),
            device_id_type=MESH,
        )

    far = [(q, dz) for q in range(4) for dz in range(4) if q or dz]

    def combine2(j):
        _, m2 = masks(j % 2)
        starts = []
        for q in range(4):
            for dz in range(4):
                yy = flip(y, m2 * (q // 2))
                starts.append(LOW - hours[base_scan(j, yy, (z - dz + 4) % 4)])
        for h in range(HOURS):
            terms = [got2_of[j][s, starts[s] + h] for s in range(16)]
            while len(terms) > 1:
                terms = [a + b for a, b in zip(terms[::2], terms[1::2])]
            out[h, j * 8 : (j + 1) * 8, :] = terms[0]

    for j in range(CHUNKS):
        for copy in step1_copies(j, False):
            copy.wait_recv()
        reduce1(j)
        for q, dz in far:
            copy2(j, q, dz, True).start()
        for k in range(SLOTS[j % 2]):
            got2_of[j][0, LOW + k] = slots_of[j][z, k]
    for j in range(CHUNKS):
        for q, dz in far:
            copy2(j, q, dz, True).wait_recv()
        combine2(j)

    tile_rows = out.shape[1]
    lane = lax.broadcasted_iota(jnp.int32, (tile_rows, 128), 1)
    owner_lane = lane
    oz, orx2, ory2 = owner_lane % 4, (owner_lane // 4) % 2, (owner_lane // 8) % 2
    oc, orx1, ory1 = (owner_lane // 16) % 2, (owner_lane // 32) % 2, owner_lane // 64

    def flip_lanes(value, bit, mask):
        return jnp.where(bit == 1, flip(value, mask), value)

    ox = flip_lanes(flip_lanes(jnp.full_like(lane, x), orx1, 1), orx2, 3)
    oy = flip_lanes(flip_lanes(jnp.full_like(lane, y), ory1, 1), ory2, 3)
    owner = (oz * 4 + (oy // 2) * 2 + oc) * 8 + (oy % 2) * 4 + ox
    share = jnp.zeros((128, 128), jnp.float32)
    for g in range(2):
        value = jnp.where(lane % 16 == HOURS, float(SEG), 0.0)
        for h in range(HOURS):
            total = jnp.sum(out[h, :, g * 128 : (g + 1) * 128], axis=1, keepdims=True)
            value = jnp.where(lane % 16 == h, total, value)
        names = ids[:, g : g + 1]
        value = jnp.where(lane // 16 == names % 8, value, 0.0)
        chosen = jnp.where(owner == names // 8, 1.0, 0.0)
        share = share + lax.dot_general(
            chosen, value, (((0,), (0,)), ((), ())),
            precision=lax.Precision.HIGHEST, preferred_element_type=jnp.float32,
        )
    part[...] = share.reshape(8, 16, 128)

    def bcopy1(ry1, rx1, tc, sc):
        return pltpu.make_async_remote_copy(
            src_ref=part.at[(ry1 * 2 + rx1) * 2 + tc],
            dst_ref=part_got.at[(ry1 * 2 + rx1) * 2 + sc],
            send_sem=bsend1.at[(ry1 * 2 + rx1) * 2 + tc],
            recv_sem=brecv1.at[(ry1 * 2 + rx1) * 2 + sc],
            device_id=device(flip(x, rx1), flip(y, ry1), z, tc),
            device_id_type=MESH,
        )

    for ry1, rx1 in quads:
        for core in range(2):
            bcopy1(ry1, rx1, core, c).start()
    bcopy1(0, 0, 1 - c, c).start()
    summed = part[c]
    for ry1, rx1 in quads:
        for core in range(2):
            bcopy1(ry1, rx1, c, core).wait_recv()
            summed = summed + part_got[(ry1 * 2 + rx1) * 2 + core]
    bcopy1(0, 0, c, 1 - c).wait_recv()
    summed = summed + part_got[1 - c]
    part_sum[...] = summed.reshape(2, 8, 128)

    def bcopy2(q, dz):
        target_z = (z + dz) % 4
        return pltpu.make_async_remote_copy(
            src_ref=part_sum.at[q // 2],
            dst_ref=part_last.at[q * 4 + dz],
            send_sem=bsend2.at[q * 4 + dz],
            recv_sem=brecv2.at[q * 4 + dz],
            device_id=device(flip(x, 3 * (q % 2)), flip(y, 3 * (q // 2)), target_z, c),
            device_id_type=MESH,
        )

    for q, dz in far:
        bcopy2(q, dz).start()
    final = part_sum[0, pl.ds(z, 1), :]
    for q, dz in far:
        bcopy2(q, dz).wait_recv()
        final = final + part_last[q * 4 + dz, pl.ds((q % 2) * 4 + z, 1), :]

    lane8 = lax.broadcasted_iota(jnp.int32, (8, 128), 1)
    row8 = lax.broadcasted_iota(jnp.int32, (8, 128), 0)
    spread = jnp.where(lane8 // 16 == row8, jnp.broadcast_to(final, (8, 128)), 0.0)
    lane_in = lax.broadcasted_iota(jnp.int32, (128, 128), 0)
    lane_out = lax.broadcasted_iota(jnp.int32, (128, 128), 1)
    pick = jnp.where(lane_in % 16 == lane_out, 1.0, 0.0)
    table = jnp.dot(spread, pick, precision=lax.Precision.HIGHEST, preferred_element_type=jnp.float32)
    depth[...] = (table / table[:, HOURS : HOURS + 1])[:, :HOURS]

    for j in range(CHUNKS):
        for copy in step1_copies(j, True):
            copy.wait_send()
        for q, dz in far:
            copy2(j, q, dz, True).wait_send()
    for ry1, rx1 in quads:
        for core in range(2):
            bcopy1(ry1, rx1, core, c).wait_send()
    bcopy1(0, 0, 1 - c, c).wait_send()
    for q, dz in far:
        bcopy2(q, dz).wait_send()


def body(reflectivity, scan_hour, basin_ids):
    vmem = pltpu.VMEM
    bands = [vmem((16, SLOTS[j % 2], 8, 256), jnp.float32) for j in range(CHUNKS)]
    padded = [vmem((16, HOURS + LOW, 8, 256), jnp.float32) for j in range(CHUNKS)]
    dma = pltpu.SemaphoreType.DMA
    return pl.pallas_call(
        kernel,
        out_shape=(
            jax.ShapeDtypeStruct((HOURS, 32, 256), jnp.float32),
            jax.ShapeDtypeStruct((8, HOURS), jnp.float32),
        ),
        in_specs=[
            pl.BlockSpec(memory_space=pl.ANY),
            pl.BlockSpec(memory_space=pltpu.SMEM),
            pl.BlockSpec(memory_space=pltpu.VMEM),
        ],
        out_specs=(pl.BlockSpec(memory_space=pltpu.VMEM), pl.BlockSpec(memory_space=pltpu.VMEM)),
        scratch_shapes=[
            vmem((CHUNKS, 2, 2, 16, 2, 8, 256), jnp.float32),
            vmem((CHUNKS, 2, 2, 2, 16, 8, 256), jnp.float32),
            *bands,
            *padded,
            vmem((8, 16, 128), jnp.float32),
            vmem((8, 16, 128), jnp.float32),
            vmem((2, 8, 128), jnp.float32),
            vmem((16, 8, 128), jnp.float32),
            dma((CHUNKS,)),
            dma((CHUNKS, 8)),
            dma((CHUNKS, 8)),
            dma((CHUNKS, 16)),
            dma((CHUNKS, 16)),
            dma((8,)),
            dma((8,)),
            dma((16,)),
            dma((16,)),
        ],
        compiler_params=pltpu.CompilerParams(collective_id=0, has_side_effects=True, vmem_limit_bytes=56 * 1024 * 1024),
    )(reflectivity.reshape(4, 2, 2, 4, 8, 2048), scan_hour, basin_ids)


def solution(mesh):
    placed = (P(("row", "col"), None, None), P(), P("row", "col"))
    return jax.shard_map(
        body,
        mesh=mesh,
        in_specs=placed,
        out_specs=(P(None, "row", "col"), P(("row", "col"), None)),
        check_vma=False,
    )
```

time: 151 us -> 74.1 us (0.49)
  Pallas kernels: 0 us -> 68.8 us
  blocking collectives: 67.1 us -> 0 us
  waiting for transfers between devices: 52 us -> 0 us
  starting transfers between devices: 12 us -> 0 us
  local copies, waits for them, and re-layouts: 12.6 us -> 4.39 us
  other arithmetic: 4.35 us -> 0 us
  matrix products: 2.14 us -> 0 us
    pallas_call x0 -> x1, Pallas kernels: none -> 68.8 us  [body(): pl.pallas_call(kernel, out_shape=(jax.ShapeDtypeStruct((HOURS, 32, 256),...]
    unnamed x1 -> x0, blocking collectives: 67.1 us -> none
    all_to_all x1 -> x0, waiting for transfers between devices: 52 us -> none  [body(): lax.all_to_all(blocks, ('row', 'col'), split_axis=1, concat_axis=0, tiled...]
    all_to_all x1 -> x0, starting transfers between devices: 12 us -> none  [body(): lax.all_to_all(blocks, ('row', 'col'), split_axis=1, concat_axis=0, tiled...]
    div x2 -> x0, other arithmetic: 3.77 us -> none  [the longest x1 3.1 us: rain_depth(): return jnp.exp(reflect * slope_db - offset_zr) / 12.0]
    unnamed x9 -> x3, local copies, waits for them, and re-layouts: 7.79 us -> 4.39 us
    transpose x1 -> x0, local copies, waits for them, and re-layouts: 3.28 us -> none  [body(): blocks.transpose(0, 1, 3, 2, 4)]
    dot_general x2 -> x0, matrix products: 2.14 us -> none  [the longest x1 1.47 us: body(): jnp.dot(selector, pixels, precision=lax.Precision.HIGHEST, preferred_elem...]
  transfers between devices with their start and end apart: 1 -> 0, of which waited for: 1 -> 0; matrix products, arithmetic and copies ran while one was open for 0% -> 0% of each run, Pallas kernels for 0% -> 0%
where the time goes in v1:
time: 74.1 us; the launch traced here: 73.9 us
  Pallas kernels  68.8 us (93%)
  local copies, waits for them, and re-layouts  4.39 us (6%)
    pallas_call x1, Pallas kernels, body(): pl.pallas_call(kernel, out_shape=(jax.ShapeDtypeStruct((HOURS, 32, 256),...  68.8 us
    unnamed x3, local copies, waits for them, and re-layouts  4.39 us

profile of v1, /device:TPU:1, one launch (start us, length us, event | category | flops | bytes accessed | tf_op | source)
XLA Modules:
  0.0 73.9 jit_solution(15736775059359247760)
XLA Ops:
  0.6 1.4 %copy.5.ids = s32[32,2]{1,0:T(8,128)} copy(s32[32,2]{0,1:T(2,128)} %param.5) | data formatting | bytes 512 | tf_op args[2]
  2.0 68.8 %shard_map.50 = (f32[12,32,256]{2,1,0:T(8,128)}, f32[8,12]{1,0:T(8,128)}) custom-call(f32[4,2,2,4,8,2048]{5,4,3,2,1,0:T(8,128)} %bitcast.1, s32[128]{0:T(128)} %hours.1, s32[32,2]{1,0:T(8,128)} %copy.5.ids), custom_call_target="tpu_custom_call" | custom-call | tf_op jit(solution)/shard_map/pallas_call | solution.py:301
  70.8 1.8 %copy.8 = f32[12,32,256]{2,1,0:T(8,128)} copy(f32[12,32,256]{2,1,0:T(8,128)} %get-tuple-element.4) | data formatting | bytes 786432
  72.6 1.3 %copy.9 = f32[8,12]{1,0:T(8,128)} copy(f32[8,12]{1,0:T(8,128)} %get-tuple-element.5) | data formatting | bytes 768

commit v2 on v0

v2 whole, which is shorter than its diff:
```python
import math

import jax
import jax.numpy as jnp
from jax import lax
from jax.experimental import pallas as pl
from jax.experimental.pallas import tpu as pltpu
from jax.sharding import PartitionSpec as P

MESH = pl.DeviceIdType.MESH
SEG = 128
HOURS = 12
BANDS = 4
CHUNKS = 8
SLOTS = (4, 5)
LOW = 11
LOG2E = 1.0 / math.log(2.0)
SCALE = math.log(10.0) / 16.0 * LOG2E
SHIFT = (math.log(200.0) / 1.6 + math.log(12.0)) * LOG2E


def rain_depth(reflect):
    return jnp.exp2(reflect * SCALE - SHIFT)


def flip(value, mask):
    if mask == 0:
        return value
    if mask == 1:
        return value + 1 - 2 * (value % 2)
    if mask == 2:
        return (value + 2) % 4
    return 3 - value


def masks(parity):
    return (1, 3) if parity == 0 else (3, 1)


def device(x, y, z, c):
    return (z * 4 + (y // 2) * 2 + c, (y % 2) * 4 + x)


def kernel(refl, hours, ids, out, table_out, *scratch):
    src, got1 = scratch[:2]
    slots_of, gotz, sumz, gotq = (scratch[2 + CHUNKS * i : 2 + CHUNKS * (i + 1)] for i in range(4))
    (
        part, part_got, part_sum, part_last,
        load_sem, send1, recv1, sendz, recvz, sendq, recvq, bsend1, brecv1, bsend2, brecv2, bsend3, brecv3,
    ) = scratch[2 + CHUNKS * 4 :]
    row, col = lax.axis_index("row"), lax.axis_index("col")
    z, c = row // 4, row % 2
    y, x = ((row // 2) % 2) * 2 + col // 4, col % 4

    for ch in range(CHUNKS):
        m1, m2 = masks(ch % 2)
        for ry1 in range(2):
            for rx1 in range(2):
                for q in range(4):
                    dy = flip(y, (m1 * ry1) ^ (m2 * (q // 2)))
                    dx = flip(x, (m1 * rx1) ^ (m2 * (q % 2)))
                    lanes = pl.ds(pl.multiple_of(((dy % 2) * 4 + dx) * 256 + (ch % 2) * 128, 128), 128)
                    pltpu.make_async_copy(
                        refl.at[:, dy // 2, :, ch // 2, :, lanes],
                        src.at[ch, ry1, rx1, :, q],
                        load_sem.at[ch],
                    ).start()

    barrier = pltpu.get_barrier_semaphore()
    quads = [(0, 1), (1, 0), (1, 1)]
    peers = [device(x, y, z, 1 - c)]
    for mask in (1, 3):
        for ry, rx in quads:
            for core in range(2):
                peers.append(device(flip(x, mask * rx), flip(y, mask * ry), z, core))
    for dz in (1, 2, 3):
        peers.append(device(x, y, (z + dz) % 4, c))
    for peer in peers:
        pl.semaphore_signal(barrier, inc=1, device_id=peer, device_id_type=MESH)

    for ch in range(CHUNKS):
        empty = jnp.zeros((4, 8, 128), jnp.float32)
        buf, slots = gotz[ch], SLOTS[ch % 2]

        @pl.loop(0, 4)
        def _(s):
            for k in range(HOURS + LOW):
                if not LOW <= k < LOW + slots:
                    buf[s, k] = empty

    pl.semaphore_wait(barrier, len(peers))

    def copy1(ch, ry1, rx1, tc, sc):
        m1, _ = masks(ch % 2)
        return pltpu.make_async_remote_copy(
            src_ref=src.at[ch, ry1, rx1, :, :, tc],
            dst_ref=got1.at[ch, ry1, rx1, sc],
            send_sem=send1.at[ch, (ry1 * 2 + rx1) * 2 + tc],
            recv_sem=recv1.at[ch, (ry1 * 2 + rx1) * 2 + sc],
            device_id=device(flip(x, m1 * rx1), flip(y, m1 * ry1), z, tc),
            device_id_type=MESH,
        )

    def step1_copies(ch, mine):
        found = []
        for ry1, rx1 in quads:
            for core in range(2):
                found.append(copy1(ch, ry1, rx1, core, c) if mine else copy1(ch, ry1, rx1, c, core))
        found.append(copy1(ch, 0, 0, 1 - c, c) if mine else copy1(ch, 0, 0, c, 1 - c))
        return found

    def base_scan(ch, zz):
        return zz * 32 + (y // 2) * 16 if ch % 2 == 0 else zz * 32

    def reduce1(ch):
        m1, _ = masks(ch % 2)
        slots = SLOTS[ch % 2]
        first = hours[base_scan(ch, z)]
        weights = []
        for ry1 in range(2):
            for rx1 in range(2):
                for core in range(2):
                    yy, xx = flip(y, m1 * ry1), flip(x, m1 * rx1)
                    cc = core if ry1 + rx1 else (c if core == 0 else 1 - c)
                    hour = hours[z * 32 + (yy // 2) * 16 + cc * 8 + (yy % 2) * 4 + xx]
                    weights.append([jnp.where(hour - first == k, 1.0, 0.0).astype(jnp.float32) for k in range(slots)])

        @pl.loop(0, 4)
        def _(zt):
            for part_q in (0, 2):
                pair = pl.ds(part_q, 2)
                total = [None] * slots
                n = 0
                for ry1 in range(2):
                    for rx1 in range(2):
                        for core in range(2):
                            if ry1 + rx1:
                                raw = got1[ch, ry1, rx1, core, zt, pair]
                            elif core == 0:
                                raw = src[ch, 0, 0, zt, pair, c]
                            else:
                                raw = got1[ch, 0, 0, 1 - c, zt, pair]
                            value = rain_depth(raw)
                            for k in range(slots):
                                term = value * weights[n][k]
                                total[k] = term if total[k] is None else total[k] + term
                            n += 1
                for k in range(slots):
                    slots_of[ch][zt, k, pair] = total[k]

    def copyz(ch, dz):
        target_z = (z + dz) % 4
        return pltpu.make_async_remote_copy(
            src_ref=slots_of[ch].at[target_z],
            dst_ref=gotz[ch].at[dz, pl.ds(LOW, SLOTS[ch % 2])],
            send_sem=sendz.at[ch, dz],
            recv_sem=recvz.at[ch, dz],
            device_id=device(x, y, target_z, c),
            device_id_type=MESH,
        )

    def combinez(ch):
        starts = [LOW - hours[base_scan(ch, (z - dz + 4) % 4)] for dz in range(4)]
        for h in range(HOURS):
            terms = [gotz[ch][dz, starts[dz] + h] for dz in range(4)]
            sumz[ch][:, h] = (terms[0] + terms[1]) + (terms[2] + terms[3])

    def copyq(ch, q):
        _, m2 = masks(ch % 2)
        return pltpu.make_async_remote_copy(
            src_ref=sumz[ch].at[q],
            dst_ref=gotq[ch].at[q - 1],
            send_sem=sendq.at[ch, q],
            recv_sem=recvq.at[ch, q],
            device_id=device(flip(x, m2 * (q % 2)), flip(y, m2 * (q // 2)), z, c),
            device_id_type=MESH,
        )

    for ch in range(CHUNKS):
        pltpu.make_async_copy(src.at[ch], src.at[ch], load_sem.at[ch]).wait()
        for copy in step1_copies(ch, True):
            copy.start()

    def first(pair):
        for ch in (2 * pair, 2 * pair + 1):
            for copy in step1_copies(ch, False):
                copy.wait_recv()
            reduce1(ch)
            for dz in (2, 1, 3):
                copyz(ch, dz).start()
            for k in range(SLOTS[ch % 2]):
                gotz[ch][0, LOW + k] = slots_of[ch][z, k]

    def second(pair):
        for ch in (2 * pair, 2 * pair + 1):
            for dz in (1, 2, 3):
                copyz(ch, dz).wait_recv()
            combinez(ch)
            for q in (3, 1, 2):
                copyq(ch, q).start()

    def third(pair):
        for ch in (2 * pair, 2 * pair + 1):
            for q in (1, 2, 3):
                copyq(ch, q).wait_recv()
            j, half = ch // 2, ch % 2
            for h in range(HOURS):
                out[h, j * 8 : (j + 1) * 8, half * 128 : (half + 1) * 128] = (
                    (sumz[ch][0, h] + gotq[ch][0, h]) + (gotq[ch][1, h] + gotq[ch][2, h])
                )

    for pair in range(BANDS + 2):
        if pair < BANDS:
            first(pair)
        if 1 <= pair <= BANDS:
            second(pair - 1)
        if pair >= 2:
            third(pair - 2)

    tile_rows = out.shape[1]
    lane = lax.broadcasted_iota(jnp.int32, (tile_rows, 128), 1)
    rank = lax.broadcasted_iota(jnp.int32, (128, tile_rows), 0)
    oz, orx2, ory2 = rank % 4, (rank // 4) % 2, (rank // 8) % 2
    oc, orx1, ory1 = (rank // 16) % 2, (rank // 32) % 2, rank // 64

    def flip_each(value, bit, mask):
        return jnp.where(bit == 1, flip(value, mask), value)

    ox = flip_each(flip_each(jnp.full_like(rank, x), orx1, 1), orx2, 3)
    oy = flip_each(flip_each(jnp.full_like(rank, y), ory1, 1), ory2, 3)
    owner = (oz * 4 + (oy // 2) * 2 + oc) * 8 + (oy % 2) * 4 + ox
    square = (tile_rows, tile_rows)
    diagonal = lax.broadcasted_iota(jnp.int32, square, 0) == lax.broadcasted_iota(jnp.int32, square, 1)
    share = jnp.zeros((128, 128), jnp.float32)
    for g in range(2):
        value = jnp.where(lane % 16 == HOURS, float(SEG), 0.0)
        for h in range(HOURS):
            total = jnp.sum(out[h, :, g * 128 : (g + 1) * 128], axis=1, keepdims=True)
            value = jnp.where(lane % 16 == h, total, value)
        names = ids[g : g + 1, :]
        place = (names % 8).astype(jnp.float32)
        place = jnp.sum(jnp.where(diagonal, place, 0.0), axis=1, keepdims=True)
        value = jnp.where((lane // 16).astype(jnp.float32) == place, value, 0.0)
        chosen = jnp.where(owner == names // 8, 1.0, 0.0)
        share = share + jnp.dot(
            chosen, value, precision=lax.Precision.HIGHEST, preferred_element_type=jnp.float32
        )
    part[...] = share.reshape(8, 16, 128)

    def bcopy1(ry1, rx1, tc, sc):
        return pltpu.make_async_remote_copy(
            src_ref=part.at[(ry1 * 2 + rx1) * 2 + tc],
            dst_ref=part_got.at[(ry1 * 2 + rx1) * 2 + sc],
            send_sem=bsend1.at[(ry1 * 2 + rx1) * 2 + tc],
            recv_sem=brecv1.at[(ry1 * 2 + rx1) * 2 + sc],
            device_id=device(flip(x, rx1), flip(y, ry1), z, tc),
            device_id_type=MESH,
        )

    for ry1, rx1 in quads:
        for core in range(2):
            bcopy1(ry1, rx1, core, c).start()
    bcopy1(0, 0, 1 - c, c).start()
    summed = part[c]
    for ry1, rx1 in quads:
        for core in range(2):
            bcopy1(ry1, rx1, c, core).wait_recv()
            summed = summed + part_got[(ry1 * 2 + rx1) * 2 + core]
    bcopy1(0, 0, c, 1 - c).wait_recv()
    summed = summed + part_got[1 - c]
    part_sum[0] = summed

    def bcopy2(dz):
        return pltpu.make_async_remote_copy(
            src_ref=part_sum.at[0],
            dst_ref=part_last.at[dz],
            send_sem=bsend2.at[dz],
            recv_sem=brecv2.at[dz],
            device_id=device(x, y, (z + dz) % 4, c),
            device_id_type=MESH,
        )

    def bcopy3(q):
        return pltpu.make_async_remote_copy(
            src_ref=part_sum.at[1],
            dst_ref=part_last.at[3 + q],
            send_sem=bsend3.at[q],
            recv_sem=brecv3.at[q],
            device_id=device(flip(x, 3 * (q % 2)), flip(y, 3 * (q // 2)), z, c),
            device_id_type=MESH,
        )

    for dz in (1, 2, 3):
        bcopy2(dz).start()
    for dz in (1, 2, 3):
        bcopy2(dz).wait_recv()
        summed = summed + part_last[dz]
    part_sum[1] = summed
    for q in (1, 2, 3):
        bcopy3(q).start()
    final = part_sum[1, pl.ds(z, 1), :]
    for q in (1, 2, 3):
        bcopy3(q).wait_recv()
        final = final + part_last[3 + q, pl.ds(q * 4 + z, 1), :]

    lane8 = lax.broadcasted_iota(jnp.int32, (8, 128), 1)
    row8 = lax.broadcasted_iota(jnp.int32, (8, 128), 0)
    spread = jnp.where(lane8 // 16 == row8, jnp.broadcast_to(final, (8, 128)), 0.0)
    lane_in = lax.broadcasted_iota(jnp.int32, (128, 128), 0)
    lane_out = lax.broadcasted_iota(jnp.int32, (128, 128), 1)
    pick = jnp.where(lane_in % 16 == lane_out, 1.0, 0.0)
    table_out[...] = jnp.dot(spread, pick, precision=lax.Precision.HIGHEST, preferred_element_type=jnp.float32)

    for ch in range(CHUNKS):
        for copy in step1_copies(ch, True):
            copy.wait_send()
        for dz in (1, 2, 3):
            copyz(ch, dz).wait_send()
        for q in (1, 2, 3):
            copyq(ch, q).wait_send()
    for ry1, rx1 in quads:
        for core in range(2):
            bcopy1(ry1, rx1, core, c).wait_send()
    bcopy1(0, 0, 1 - c, c).wait_send()
    for n in (1, 2, 3):
        bcopy2(n).wait_send()
        bcopy3(n).wait_send()


def finish(hourly, table, out, depth):
    out[...] = hourly[...]
    depth[...] = (table[...] / table[:, HOURS : HOURS + 1])[:, :HOURS]


def body(reflectivity, scan_hour, basin_ids):
    def vmem(*shape):
        return pltpu.VMEM(shape, jnp.float32)

    def dma(*shape):
        return pltpu.SemaphoreType.DMA(shape)

    chunks = range(CHUNKS)
    scratch = [
        vmem(CHUNKS, 2, 2, 4, 4, 2, 8, 128),
        vmem(CHUNKS, 2, 2, 2, 4, 4, 8, 128),
        *[vmem(4, SLOTS[ch % 2], 4, 8, 128) for ch in chunks],
        *[vmem(4, HOURS + LOW, 4, 8, 128) for ch in chunks],
        *[vmem(4, HOURS, 8, 128) for ch in chunks],
        *[vmem(3, HOURS, 8, 128) for ch in chunks],
        vmem(8, 16, 128), vmem(8, 16, 128), vmem(2, 16, 128), vmem(7, 16, 128),
        dma(CHUNKS), dma(CHUNKS, 8), dma(CHUNKS, 8), dma(CHUNKS, 4), dma(CHUNKS, 4), dma(CHUNKS, 4), dma(CHUNKS, 4),
        dma(8), dma(8), dma(4), dma(4), dma(4), dma(4),
    ]
    block = pl.BlockSpec(memory_space=pltpu.VMEM)
    hourly, table = pl.pallas_call(
        kernel,
        out_shape=(
            jax.ShapeDtypeStruct((HOURS, 32, 256), jnp.float32),
            jax.ShapeDtypeStruct((8, 128), jnp.float32),
        ),
        in_specs=[pl.BlockSpec(memory_space=pl.ANY), pl.BlockSpec(memory_space=pltpu.SMEM), block],
        out_specs=(block, block),
        scratch_shapes=scratch,
        compiler_params=pltpu.CompilerParams(
            collective_id=0, has_side_effects=True, vmem_limit_bytes=52 * 1024 * 1024
        ),
    )(reflectivity.reshape(4, 2, 2, BANDS, 8, 2048), scan_hour, basin_ids.T)
    return pl.pallas_call(
        finish,
        out_shape=(
            jax.ShapeDtypeStruct((HOURS, 32, 256), jnp.float32),
            jax.ShapeDtypeStruct((8, HOURS), jnp.float32),
        ),
        in_specs=[block, block],
        out_specs=(block, block),
        compiler_params=pltpu.CompilerParams(vmem_limit_bytes=8 * 1024 * 1024),
    )(hourly, table)


def solution(mesh):
    placed = (P(("row", "col"), None, None), P(), P("row", "col"))
    return jax.shard_map(
        body,
        mesh=mesh,
        in_specs=placed,
        out_specs=(P(None, "row", "col"), P(("row", "col"), None)),
        check_vma=False,
    )
```

time: 151 us -> 65.4 us (0.43)
  blocking collectives: 67.1 us -> 0 us
  Pallas kernels: 0 us -> 62.5 us
  waiting for transfers between devices: 52 us -> 0 us
  starting transfers between devices: 12 us -> 0 us
  local copies, waits for them, and re-layouts: 12.6 us -> 1.33 us
  other arithmetic: 4.35 us -> 0 us
  matrix products: 2.14 us -> 0 us
    unnamed x1 -> x0, blocking collectives: 67.1 us -> none
    pallas_call x0 -> x2, Pallas kernels: none -> 62.5 us  [the longest x1 61.7 us: body(): pl.pallas_call(kernel, out_shape=(jax.ShapeDtypeStruct((HOURS, 32, 256),...]
    all_to_all x1 -> x0, waiting for transfers between devices: 52 us -> none  [body(): lax.all_to_all(blocks, ('row', 'col'), split_axis=1, concat_axis=0, tiled...]
    all_to_all x1 -> x0, starting transfers between devices: 12 us -> none  [body(): lax.all_to_all(blocks, ('row', 'col'), split_axis=1, concat_axis=0, tiled...]
    unnamed x9 -> x4, local copies, waits for them, and re-layouts: 7.79 us -> 1.33 us
    div x2 -> x0, other arithmetic: 3.77 us -> none  [the longest x1 3.1 us: rain_depth(): return jnp.exp(reflect * slope_db - offset_zr) / 12.0]
    transpose x1 -> x0, local copies, waits for them, and re-layouts: 3.28 us -> none  [body(): blocks.transpose(0, 1, 3, 2, 4)]
    dot_general x2 -> x0, matrix products: 2.14 us -> none  [the longest x1 1.47 us: body(): jnp.dot(selector, pixels, precision=lax.Precision.HIGHEST, preferred_elem...]
  transfers between devices with their start and end apart: 1 -> 0, of which waited for: 1 -> 0; matrix products, arithmetic and copies ran while one was open for 0% -> 0% of each run, Pallas kernels for 0% -> 0%
where the time goes in v2:
time: 65.4 us; the launch traced here: 64.5 us
  Pallas kernels  62.5 us (96%)
  local copies, waits for them, and re-layouts  1.33 us (2%)
    pallas_call x1, Pallas kernels, body(): pl.pallas_call(kernel, out_shape=(jax.ShapeDtypeStruct((HOURS, 32, 256),...  61.7 us
    unnamed x4, local copies, waits for them, and re-layouts  1.33 us

profile of v2, /device:TPU:1, one launch (start us, length us, event | category | flops | bytes accessed | tf_op | source)
XLA Modules:
  0.0 64.5 jit_solution(16225539818936699754)
XLA Ops:
  0.6 0.0 copy-start
  0.6 0.7 %copy-done = s32[32,2]{0,1:T(2,128)S(1)} copy-done((s32[32,2]{0,1:T(2,128)S(1)}, s32[32,2]{0,1:T(2,128)}, u32[]{:S(2)}) %copy-start) | copy-done | bytes 280
  1.3 0.0 copy-start.1
  1.3 0.7 %copy-done.1 = s32[128]{0:T(128)S(1)} copy-done((s32[128]{0:T(128)S(1)}, s32[128]{0:T(128)}, u32[]{:S(2)}) %copy-start.1) | copy-done | bytes 536
  2.0 61.7 %shard_map.50 = (f32[12,32,256]{2,1,0:T(8,128)S(1)}, f32[8,128]{1,0:T(8,128)S(1)}) custom-call(f32[4,2,2,4,8,2048]{5,4,3,2,1,0:T(8,128)} %bitcast.3, s32[128]{0:T(128)S(1)} %copy-done.1, s32[2,32]{1,0:T(2,128)S(1)} %bitcast.2), custom_call_target="tpu_custom_call" | custom-call | tf_op jit(solution)/shard_map/pallas_call | solution.py:355
  63.7 0.8 %shard_map.51 = (f32[12,32,256]{2,1,0:T(8,128)}, f32[8,12]{1,0:T(8,128)}) custom-call(f32[12,32,256]{2,1,0:T(8,128)S(1)} %get-tuple-element.4.hourly, f32[8,128]{1,0:T(8,128)S(1)} %get-tuple-element.5.table), custom_call_target="tpu_custom_call" | custom-call | tf_op jit(solution)/shard_map/pallas_call | solution.py:368
Async XLA Ops:
  0.6 0.7 %copy-start = (s32[32,2]{0,1:T(2,128)S(1)}, s32[32,2]{0,1:T(2,128)}, u32[]{:S(2)}) copy-start(s32[32,2]{0,1:T(2,128)} %param.5) | copy-start | bytes 772
  1.3 0.7 %copy-start.1 = (s32[128]{0:T(128)S(1)}, s32[128]{0:T(128)}, u32[]{:S(2)}) copy-start(s32[128]{0:T(128)} %hours.1) | copy-start | bytes 1540

commit v3 on v2

--- a/solution.py
+++ b/solution.py
@@ -45,8 +45,9 @@
     src, got1 = scratch[:2]
     slots_of, gotz, sumz, gotq = (scratch[2 + CHUNKS * i : 2 + CHUNKS * (i + 1)] for i in range(4))
     (
-        part, part_got, part_sum, part_last,
-        load_sem, send1, recv1, sendz, recvz, sendq, recvq, bsend1, brecv1, bsend2, brecv2, bsend3, brecv3,
+        own_seg, got_seg, seg_hours, got_hours, seg_pack, got_pack, part, part_got, part_sum, part_last, row_sum, row_got,
+        load_sem, send1, recv1, sendz, recvz, sendq, recvq, esend1, erecv1, esend2, erecv2, esend3, erecv3,
+        bsend1, brecv1, bsend2, brecv2, bsend3, brecv3,
     ) = scratch[2 + CHUNKS * 4 :]
     row, col = lax.axis_index("row"), lax.axis_index("col")
     z, c = row // 4, row % 2
@@ -176,10 +177,14 @@
             device_id_type=MESH,
         )
 
-    for ch in range(CHUNKS):
-        pltpu.make_async_copy(src.at[ch], src.at[ch], load_sem.at[ch]).wait()
-        for copy in step1_copies(ch, True):
-            copy.start()
+    def loaded(*which):
+        for ch in which:
+            pltpu.make_async_copy(src.at[ch], src.at[ch], load_sem.at[ch]).wait()
+
+    def start1(pair):
+        for one, two in zip(step1_copies(2 * pair, True), step1_copies(2 * pair + 1, True)):
+            one.start()
+            two.start()
 
     def first(pair):
         for ch in (2 * pair, 2 * pair + 1):
@@ -209,107 +214,246 @@
                     (sumz[ch][0, h] + gotq[ch][0, h]) + (gotq[ch][1, h] + gotq[ch][2, h])
                 )
 
-    for pair in range(BANDS + 2):
-        if pair < BANDS:
-            first(pair)
-        if 1 <= pair <= BANDS:
-            second(pair - 1)
-        if pair >= 2:
-            third(pair - 2)
-
-    tile_rows = out.shape[1]
-    lane = lax.broadcasted_iota(jnp.int32, (tile_rows, 128), 1)
-    rank = lax.broadcasted_iota(jnp.int32, (128, tile_rows), 0)
-    oz, orx2, ory2 = rank % 4, (rank // 4) % 2, (rank // 8) % 2
-    oc, orx1, ory1 = (rank // 16) % 2, (rank // 32) % 2, rank // 64
-
-    def flip_each(value, bit, mask):
-        return jnp.where(bit == 1, flip(value, mask), value)
-
-    ox = flip_each(flip_each(jnp.full_like(rank, x), orx1, 1), orx2, 3)
-    oy = flip_each(flip_each(jnp.full_like(rank, y), ory1, 1), ory2, 3)
-    owner = (oz * 4 + (oy // 2) * 2 + oc) * 8 + (oy % 2) * 4 + ox
-    square = (tile_rows, tile_rows)
-    diagonal = lax.broadcasted_iota(jnp.int32, square, 0) == lax.broadcasted_iota(jnp.int32, square, 1)
-    share = jnp.zeros((128, 128), jnp.float32)
-    for g in range(2):
-        value = jnp.where(lane % 16 == HOURS, float(SEG), 0.0)
+    lane = lax.broadcasted_iota(jnp.int32, (8, 128), 1)
+
+    def own_segments():
+        def one_z(zt, totals):
+            totals = list(totals)
+            here = lane - zt * 32
+            for q in range(4):
+                for ch in range(CHUNKS):
+                    spot = here == q * 8 + ch
+                    for n in range(8):
+                        ey1, ex1, core = n // 4, (n // 2) % 2, n % 2
+                        if ch % 2 == 0:
+                            raw = src[ch, ey1, ex1, zt, q, core]
+                        else:
+                            raw = src[ch, q // 2, q % 2, zt, ey1 * 2 + ex1, core]
+                        total = jnp.sum(rain_depth(raw), axis=1, keepdims=True)
+                        totals[n] = jnp.where(spot, total, totals[n])
+            return tuple(totals)
+
+        totals = lax.fori_loop(0, 4, one_z, tuple(jnp.zeros((8, 128), jnp.float32) for _ in range(8)))
+        for n in range(8):
+            own_seg[n // 4, (n // 2) % 2, n % 2] = totals[n]
+
+    def ecopy1(ry1, rx1, tc, sc):
+        n = (ry1 * 2 + rx1) * 2
+        return pltpu.make_async_remote_copy(
+            src_ref=own_seg.at[ry1, rx1, tc],
+            dst_ref=got_seg.at[ry1, rx1, sc],
+            send_sem=esend1.at[n + tc],
+            recv_sem=erecv1.at[n + sc],
+            device_id=device(flip(x, rx1), flip(y, ry1), z, tc),
+            device_id_type=MESH,
+        )
+
+    def ecopy2(dz):
+        return pltpu.make_async_remote_copy(
+            src_ref=seg_hours,
+            dst_ref=got_hours.at[dz - 1],
+            send_sem=esend2.at[dz],
+            recv_sem=erecv2.at[dz],
+            device_id=device(x, y, (z + dz) % 4, c),
+            device_id_type=MESH,
+        )
+
+    def ecopy3(q):
+        return pltpu.make_async_remote_copy(
+            src_ref=seg_pack,
+            dst_ref=got_pack.at[q - 1],
+            send_sem=esend3.at[q],
+            recv_sem=erecv3.at[q],
+            device_id=device(flip(x, 3 * (q % 2)), flip(y, 3 * (q // 2)), z, c),
+            device_id_type=MESH,
+        )
+
+    def quad_out(copy):
+        found = [copy(ry1, rx1, core, c) for ry1, rx1 in quads for core in range(2)]
+        return found + [copy(0, 0, 1 - c, c)]
+
+    def quad_in(copy):
+        found = [copy(ry1, rx1, c, core) for ry1, rx1 in quads for core in range(2)]
+        return found + [copy(0, 0, c, 1 - c)]
+
+    def segments1():
+        loaded(*range(2, CHUNKS))
+        own_segments()
+        for copy in quad_out(ecopy1):
+            copy.start()
+
+    def segments2():
+        for copy in quad_in(ecopy1):
+            copy.wait_recv()
+        totals = [None] * HOURS
+        for ry1 in range(2):
+            for rx1 in range(2):
+                for core in range(2):
+                    yy, xx = flip(y, ry1), flip(x, rx1)
+                    if ry1 + rx1:
+                        cc, value = core, got_seg[ry1, rx1, core]
+                    elif core == 0:
+                        cc, value = c, own_seg[0, 0, c]
+                    else:
+                        cc, value = 1 - c, got_seg[0, 0, 1 - c]
+                    hour = hours[z * 32 + (yy // 2) * 16 + cc * 8 + (yy % 2) * 4 + xx]
+                    for h in range(HOURS):
+                        term = value * jnp.where(hour == h, 1.0, 0.0).astype(jnp.float32)
+                        totals[h] = term if totals[h] is None else totals[h] + term
         for h in range(HOURS):
-            total = jnp.sum(out[h, :, g * 128 : (g + 1) * 128], axis=1, keepdims=True)
-            value = jnp.where(lane % 16 == h, total, value)
-        names = ids[g : g + 1, :]
-        place = (names % 8).astype(jnp.float32)
-        place = jnp.sum(jnp.where(diagonal, place, 0.0), axis=1, keepdims=True)
-        value = jnp.where((lane // 16).astype(jnp.float32) == place, value, 0.0)
-        chosen = jnp.where(owner == names // 8, 1.0, 0.0)
-        share = share + jnp.dot(
-            chosen, value, precision=lax.Precision.HIGHEST, preferred_element_type=jnp.float32
-        )
-    part[...] = share.reshape(8, 16, 128)
+            seg_hours[h] = totals[h]
+        for dz in (2, 1, 3):
+            ecopy2(dz).start()
+
+    def segments3():
+        for dz in (1, 2, 3):
+            ecopy2(dz).wait_recv()
+        for k in range(HOURS // 4):
+            packed = jnp.zeros((8, 128), jnp.float32)
+            for h in range(4 * k, 4 * k + 4):
+                value = (seg_hours[h] + got_hours[0, h]) + (got_hours[1, h] + got_hours[2, h])
+                value = jnp.where(lane // 32 == z, value, 0.0)
+                value = value + pltpu.roll(value, 64, 1)
+                value = value + pltpu.roll(value, 32, 1)
+                packed = jnp.where(lane // 32 == h % 4, value, packed)
+            seg_pack[k] = packed
+        for q in (3, 1, 2):
+            ecopy3(q).start()
+
+    def shares():
+        for q in (1, 2, 3):
+            ecopy3(q).wait_recv()
+        table = []
+        for k in range(HOURS // 4):
+            value = seg_pack[k]
+            for q in (1, 2, 3):
+                value = value + pltpu.roll(got_pack[q - 1, k], 128 - 8 * q, 1)
+            table.append(value)
+        tile_rows = out.shape[1]
+        wide = lax.broadcasted_iota(jnp.int32, (tile_rows, 128), 1)
+        rank = lax.broadcasted_iota(jnp.int32, (128, tile_rows), 0)
+        oz, orx2, ory2 = rank % 4, (rank // 4) % 2, (rank // 8) % 2
+        oc, orx1, ory1 = (rank // 16) % 2, (rank // 32) % 2, rank // 64
+
+        def flip_each(value, bit, mask):
+            return jnp.where(bit == 1, flip(value, mask), value)
+
+        ox = flip_each(flip_each(jnp.full_like(rank, x), orx1, 1), orx2, 3)
+        oy = flip_each(flip_each(jnp.full_like(rank, y), ory1, 1), ory2, 3)
+        owner = (oz * 4 + (oy // 2) * 2 + oc) * 8 + (oy % 2) * 4 + ox
+        square = (tile_rows, tile_rows)
+        diagonal = lax.broadcasted_iota(jnp.int32, square, 0) == lax.broadcasted_iota(jnp.int32, square, 1)
+        share = jnp.zeros((128, 128), jnp.float32)
+        for g in range(2):
+            bands = []
+            for j in range(BANDS):
+                value = jnp.where(lane % 16 == HOURS, float(SEG), 0.0)
+                for h in range(HOURS):
+                    at = (h % 4) * 32 + j * 2 + g
+                    value = jnp.where(lane % 16 == h, table[h // 4][:, at : at + 1], value)
+                bands.append(value)
+            value = jnp.concatenate(bands, axis=0)
+            names = ids[g : g + 1, :]
+            place = (names % 8).astype(jnp.float32)
+            place = jnp.sum(jnp.where(diagonal, place, 0.0), axis=1, keepdims=True)
+            value = jnp.where((wide // 16).astype(jnp.float32) == place, value, 0.0)
+            chosen = jnp.where(owner == names // 8, 1.0, 0.0)
+            share = share + jnp.dot(
+                chosen, value, precision=lax.Precision.HIGHEST, preferred_element_type=jnp.float32
+            )
+        part[...] = share.reshape(8, 16, 128)
+        for copy in quad_out(bcopy1):
+            copy.start()
 
     def bcopy1(ry1, rx1, tc, sc):
-        return pltpu.make_async_remote_copy(
-            src_ref=part.at[(ry1 * 2 + rx1) * 2 + tc],
-            dst_ref=part_got.at[(ry1 * 2 + rx1) * 2 + sc],
-            send_sem=bsend1.at[(ry1 * 2 + rx1) * 2 + tc],
-            recv_sem=brecv1.at[(ry1 * 2 + rx1) * 2 + sc],
+        n = (ry1 * 2 + rx1) * 2
+        return pltpu.make_async_remote_copy(
+            src_ref=part.at[n + tc],
+            dst_ref=part_got.at[n + sc],
+            send_sem=bsend1.at[n + tc],
+            recv_sem=brecv1.at[n + sc],
             device_id=device(flip(x, rx1), flip(y, ry1), z, tc),
             device_id_type=MESH,
         )
 
-    for ry1, rx1 in quads:
-        for core in range(2):
-            bcopy1(ry1, rx1, core, c).start()
-    bcopy1(0, 0, 1 - c, c).start()
-    summed = part[c]
-    for ry1, rx1 in quads:
-        for core in range(2):
-            bcopy1(ry1, rx1, c, core).wait_recv()
-            summed = summed + part_got[(ry1 * 2 + rx1) * 2 + core]
-    bcopy1(0, 0, c, 1 - c).wait_recv()
-    summed = summed + part_got[1 - c]
-    part_sum[0] = summed
-
-    def bcopy2(dz):
-        return pltpu.make_async_remote_copy(
-            src_ref=part_sum.at[0],
-            dst_ref=part_last.at[dz],
-            send_sem=bsend2.at[dz],
-            recv_sem=brecv2.at[dz],
+    def bcopy2(q):
+        return pltpu.make_async_remote_copy(
+            src_ref=part_sum,
+            dst_ref=part_last.at[q - 1],
+            send_sem=bsend2.at[q],
+            recv_sem=brecv2.at[q],
+            device_id=device(flip(x, 3 * (q % 2)), flip(y, 3 * (q // 2)), z, c),
+            device_id_type=MESH,
+        )
+
+    def bcopy3(dz):
+        return pltpu.make_async_remote_copy(
+            src_ref=row_sum,
+            dst_ref=row_got.at[dz - 1],
+            send_sem=bsend3.at[dz],
+            recv_sem=brecv3.at[dz],
             device_id=device(x, y, (z + dz) % 4, c),
             device_id_type=MESH,
         )
 
-    def bcopy3(q):
-        return pltpu.make_async_remote_copy(
-            src_ref=part_sum.at[1],
-            dst_ref=part_last.at[3 + q],
-            send_sem=bsend3.at[q],
-            recv_sem=brecv3.at[q],
-            device_id=device(flip(x, 3 * (q % 2)), flip(y, 3 * (q // 2)), z, c),
-            device_id_type=MESH,
-        )
-
-    for dz in (1, 2, 3):
-        bcopy2(dz).start()
-    for dz in (1, 2, 3):
-        bcopy2(dz).wait_recv()
-        summed = summed + part_last[dz]
-    part_sum[1] = summed
-    for q in (1, 2, 3):
-        bcopy3(q).start()
-    final = part_sum[1, pl.ds(z, 1), :]
-    for q in (1, 2, 3):
-        bcopy3(q).wait_recv()
-        final = final + part_last[3 + q, pl.ds(q * 4 + z, 1), :]
-
-    lane8 = lax.broadcasted_iota(jnp.int32, (8, 128), 1)
-    row8 = lax.broadcasted_iota(jnp.int32, (8, 128), 0)
-    spread = jnp.where(lane8 // 16 == row8, jnp.broadcast_to(final, (8, 128)), 0.0)
-    lane_in = lax.broadcasted_iota(jnp.int32, (128, 128), 0)
-    lane_out = lax.broadcasted_iota(jnp.int32, (128, 128), 1)
-    pick = jnp.where(lane_in % 16 == lane_out, 1.0, 0.0)
-    table_out[...] = jnp.dot(spread, pick, precision=lax.Precision.HIGHEST, preferred_element_type=jnp.float32)
+    def shares2():
+        for copy in quad_in(bcopy1):
+            copy.wait_recv()
+        summed = part[c] + part_got[1 - c]
+        for ry1, rx1 in quads:
+            for core in range(2):
+                summed = summed + part_got[(ry1 * 2 + rx1) * 2 + core]
+        part_sum[...] = summed
+        for q in (3, 1, 2):
+            bcopy2(q).start()
+
+    def shares3():
+        for q in (1, 2, 3):
+            bcopy2(q).wait_recv()
+        row_sum[...] = jnp.zeros((8, 128), jnp.float32)
+        row_sum[0:4] = (part_sum[0:4] + part_last[0, 4:8]) + (part_last[1, 8:12] + part_last[2, 12:16])
+        for dz in (2, 1, 3):
+            bcopy3(dz).start()
+
+    def shares4():
+        final = row_sum[pl.ds(z, 1), :]
+        for dz in (1, 2, 3):
+            bcopy3(dz).wait_recv()
+        for dz in (1, 2, 3):
+            final = final + row_got[dz - 1, pl.ds(z, 1), :]
+        row8 = lax.broadcasted_iota(jnp.int32, (8, 128), 0)
+        spread = jnp.where(lane // 16 == row8, jnp.broadcast_to(final, (8, 128)), 0.0)
+        lane_in = lax.broadcasted_iota(jnp.int32, (128, 128), 0)
+        lane_out = lax.broadcasted_iota(jnp.int32, (128, 128), 1)
+        pick = jnp.where(lane_in % 16 == lane_out, 1.0, 0.0)
+        table_out[...] = jnp.dot(
+            spread, pick, precision=lax.Precision.HIGHEST, preferred_element_type=jnp.float32
+        )
+
+    loaded(0, 1)
+    start1(0)
+    segments1()
+    start1(1)
+    first(0)
+    segments2()
+    start1(2)
+    first(1)
+    segments3()
+    start1(3)
+    second(0)
+    first(2)
+    shares()
+    second(1)
+    third(0)
+    first(3)
+    shares2()
+    second(2)
+    third(1)
+    shares3()
+    second(3)
+    third(2)
+    shares4()
+    third(3)
 
     for ch in range(CHUNKS):
         for copy in step1_copies(ch, True):
@@ -318,13 +462,11 @@
             copyz(ch, dz).wait_send()
         for q in (1, 2, 3):
             copyq(ch, q).wait_send()
-    for ry1, rx1 in quads:
-        for core in range(2):
-            bcopy1(ry1, rx1, core, c).wait_send()
-    bcopy1(0, 0, 1 - c, c).wait_send()
+    for copy in quad_out(ecopy1) + quad_out(bcopy1):
+        copy.wait_send()
     for n in (1, 2, 3):
-        bcopy2(n).wait_send()
-        bcopy3(n).wait_send()
+        for small in (ecopy2, ecopy3, bcopy2, bcopy3):
+            small(n).wait_send()
 
 
 def finish(hourly, table, out, depth):
@@ -347,9 +489,11 @@
         *[vmem(4, HOURS + LOW, 4, 8, 128) for ch in chunks],
         *[vmem(4, HOURS, 8, 128) for ch in chunks],
         *[vmem(3, HOURS, 8, 128) for ch in chunks],
-        vmem(8, 16, 128), vmem(8, 16, 128), vmem(2, 16, 128), vmem(7, 16, 128),
+        vmem(2, 2, 2, 8, 128), vmem(2, 2, 2, 8, 128), vmem(HOURS, 8, 128), vmem(3, HOURS, 8, 128),
+        vmem(HOURS // 4, 8, 128), vmem(3, HOURS // 4, 8, 128),
+        vmem(8, 16, 128), vmem(8, 16, 128), vmem(16, 128), vmem(3, 16, 128), vmem(8, 128), vmem(3, 8, 128),
         dma(CHUNKS), dma(CHUNKS, 8), dma(CHUNKS, 8), dma(CHUNKS, 4), dma(CHUNKS, 4), dma(CHUNKS, 4), dma(CHUNKS, 4),
-        dma(8), dma(8), dma(4), dma(4), dma(4), dma(4),
+        dma(8), dma(8), dma(4), dma(4), dma(4), dma(4), dma(8), dma(8), dma(4), dma(4), dma(4), dma(4),
     ]
     block = pl.BlockSpec(memory_space=pltpu.VMEM)
     hourly, table = pl.pallas_call(

time: 65.4 us -> 57.6 us (0.88); the launches traced: 64.5 us -> 57.4 us
  Pallas kernels: 62.5 us -> 55.5 us
    pallas_call x1, Pallas kernels: 61.7 us -> 54.7 us  [body(): pl.pallas_call(kernel, out_shape=(jax.ShapeDtypeStruct((HOURS, 32, 256),...]
where the time goes in v3:
time: 57.6 us; the launch traced here: 57.4 us
  Pallas kernels  55.5 us (96%)
  local copies, waits for them, and re-layouts  1.33 us (2%)
  between operations  0.65 us (1%)
    pallas_call x1, Pallas kernels, body(): pl.pallas_call(kernel, out_shape=(jax.ShapeDtypeStruct((HOURS, 32, 256),...  54.7 us
    unnamed x4, local copies, waits for them, and re-layouts  1.33 us

profile of v3, /device:TPU:1, one launch (start us, length us, event | category | flops | bytes accessed | tf_op | source)
XLA Modules:
  0.0 57.4 jit_solution(12208839902003193960)
XLA Ops:
  0.6 0.0 copy-start
  0.6 0.7 %copy-done = s32[32,2]{0,1:T(2,128)S(1)} copy-done((s32[32,2]{0,1:T(2,128)S(1)}, s32[32,2]{0,1:T(2,128)}, u32[]{:S(2)}) %copy-start) | copy-done | bytes 280
  1.3 0.0 copy-start.1
  1.3 0.7 %copy-done.1 = s32[128]{0:T(128)S(1)} copy-done((s32[128]{0:T(128)S(1)}, s32[128]{0:T(128)}, u32[]{:S(2)}) %copy-start.1) | copy-done | bytes 536
  2.0 54.7 %shard_map.50 = (f32[12,32,256]{2,1,0:T(8,128)S(1)}, f32[8,128]{1,0:T(8,128)S(1)}) custom-call(f32[4,2,2,4,8,2048]{5,4,3,2,1,0:T(8,128)} %bitcast.3, s32[128]{0:T(128)S(1)} %copy-done.1, s32[2,32]{1,0:T(2,128)S(1)} %bitcast.2), custom_call_target="tpu_custom_call" | custom-call | tf_op jit(solution)/shard_map/pallas_call | solution.py:499
  56.7 0.8 %shard_map.51 = (f32[12,32,256]{2,1,0:T(8,128)}, f32[8,12]{1,0:T(8,128)}) custom-call(f32[12,32,256]{2,1,0:T(8,128)S(1)} %get-tuple-element.4.hourly, f32[8,128]{1,0:T(8,128)S(1)} %get-tuple-element.5.table), custom_call_target="tpu_custom_call" | custom-call | tf_op jit(solution)/shard_map/pallas_call | solution.py:512
Async XLA Ops:
  0.6 0.7 %copy-start = (s32[32,2]{0,1:T(2,128)S(1)}, s32[32,2]{0,1:T(2,128)}, u32[]{:S(2)}) copy-start(s32[32,2]{0,1:T(2,128)} %param.5) | copy-start | bytes 772
  1.3 0.7 %copy-start.1 = (s32[128]{0:T(128)S(1)}, s32[128]{0:T(128)}, u32[]{:S(2)}) copy-start(s32[128]{0:T(128)} %hours.1) | copy-start | bytes 1540

commit v4 on v3

--- a/solution.py
+++ b/solution.py
@@ -12,6 +12,8 @@
 HOURS = 12
 BANDS = 4
 CHUNKS = 8
+EARLY_Z = (6, 7)
+LATE_Z = (3,)
 SLOTS = (4, 5)
 LOW = 11
 LOG2E = 1.0 / math.log(2.0)
@@ -48,12 +50,26 @@
         own_seg, got_seg, seg_hours, got_hours, seg_pack, got_pack, part, part_got, part_sum, part_last, row_sum, row_got,
         load_sem, send1, recv1, sendz, recvz, sendq, recvq, esend1, erecv1, esend2, erecv2, esend3, erecv3,
         bsend1, brecv1, bsend2, brecv2, bsend3, brecv3,
-    ) = scratch[2 + CHUNKS * 4 :]
+    ) = scratch[2 + CHUNKS * 4 : len(scratch) - 3 - len(EARLY_Z)]
+    raw_z = dict(zip(EARLY_Z, scratch[len(scratch) - 3 - len(EARLY_Z) :]))
+    sendr, recvr, localr = scratch[-3:]
     row, col = lax.axis_index("row"), lax.axis_index("col")
     z, c = row // 4, row % 2
     y, x = ((row // 2) % 2) * 2 + col // 4, col % 4
 
-    for ch in range(CHUNKS):
+    barrier = pltpu.get_barrier_semaphore()
+    quads = [(0, 1), (1, 0), (1, 1)]
+    peers = [device(x, y, z, 1 - c)]
+    for mask in (1, 3):
+        for ry, rx in quads:
+            for core in range(2):
+                peers.append(device(flip(x, mask * rx), flip(y, mask * ry), z, core))
+    for dz in (1, 2, 3):
+        peers.append(device(x, y, (z + dz) % 4, c))
+    for peer in peers:
+        pl.semaphore_signal(barrier, inc=1, device_id=peer, device_id_type=MESH)
+
+    def load(ch):
         m1, m2 = masks(ch % 2)
         for ry1 in range(2):
             for rx1 in range(2):
@@ -67,34 +83,27 @@
                         load_sem.at[ch],
                     ).start()
 
-    barrier = pltpu.get_barrier_semaphore()
-    quads = [(0, 1), (1, 0), (1, 1)]
-    peers = [device(x, y, z, 1 - c)]
-    for mask in (1, 3):
-        for ry, rx in quads:
-            for core in range(2):
-                peers.append(device(flip(x, mask * rx), flip(y, mask * ry), z, core))
-    for dz in (1, 2, 3):
-        peers.append(device(x, y, (z + dz) % 4, c))
-    for peer in peers:
-        pl.semaphore_signal(barrier, inc=1, device_id=peer, device_id_type=MESH)
-
-    for ch in range(CHUNKS):
-        empty = jnp.zeros((4, 8, 128), jnp.float32)
-        buf, slots = gotz[ch], SLOTS[ch % 2]
-
-        @pl.loop(0, 4)
-        def _(s):
-            for k in range(HOURS + LOW):
-                if not LOW <= k < LOW + slots:
-                    buf[s, k] = empty
-
+    for ch in (0, 1) + EARLY_Z:
+        load(ch)
     pl.semaphore_wait(barrier, len(peers))
+
+    def clear():
+        for ch in range(CHUNKS):
+            empty = jnp.zeros(gotz[ch].shape[2:], jnp.float32)
+            buf, slots = gotz[ch], SLOTS[ch % 2]
+
+            @pl.loop(0, 4)
+            def _(s):
+                for k in range(HOURS + LOW):
+                    if not LOW <= k < LOW + slots:
+                        buf[s, k] = empty
+
 
     def copy1(ch, ry1, rx1, tc, sc):
         m1, _ = masks(ch % 2)
-        return pltpu.make_async_remote_copy(
-            src_ref=src.at[ch, ry1, rx1, :, :, tc],
+        block = raw_z[ch].at[:, ry1, rx1, :, tc] if ch in EARLY_Z else src.at[ch, ry1, rx1, :, :, tc]
+        return pltpu.make_async_remote_copy(
+            src_ref=block,
             dst_ref=got1.at[ch, ry1, rx1, sc],
             send_sem=send1.at[ch, (ry1 * 2 + rx1) * 2 + tc],
             recv_sem=recv1.at[ch, (ry1 * 2 + rx1) * 2 + sc],
@@ -102,12 +111,11 @@
             device_id_type=MESH,
         )
 
-    def step1_copies(ch, mine):
+    def step1_copies(ch, mine, which=slice(0, 7)):
+        partners = [(ry1, rx1, core) for ry1, rx1 in quads for core in range(2)]
         found = []
-        for ry1, rx1 in quads:
-            for core in range(2):
-                found.append(copy1(ch, ry1, rx1, core, c) if mine else copy1(ch, ry1, rx1, c, core))
-        found.append(copy1(ch, 0, 0, 1 - c, c) if mine else copy1(ch, 0, 0, c, 1 - c))
+        for ry1, rx1, core in (partners + [(0, 0, 1 - c)])[which]:
+            found.append(copy1(ch, ry1, rx1, core, c) if mine else copy1(ch, ry1, rx1, c, core))
         return found
 
     def base_scan(ch, zz):
@@ -116,18 +124,25 @@
     def reduce1(ch):
         m1, _ = masks(ch % 2)
         slots = SLOTS[ch % 2]
-        first = hours[base_scan(ch, z)]
-        weights = []
-        for ry1 in range(2):
-            for rx1 in range(2):
-                for core in range(2):
-                    yy, xx = flip(y, m1 * ry1), flip(x, m1 * rx1)
-                    cc = core if ry1 + rx1 else (c if core == 0 else 1 - c)
-                    hour = hours[z * 32 + (yy // 2) * 16 + cc * 8 + (yy % 2) * 4 + xx]
-                    weights.append([jnp.where(hour - first == k, 1.0, 0.0).astype(jnp.float32) for k in range(slots)])
+
+        def weights_of(zz):
+            first = hours[base_scan(ch, zz)]
+            weights = []
+            for ry1 in range(2):
+                for rx1 in range(2):
+                    for core in range(2):
+                        yy, xx = flip(y, m1 * ry1), flip(x, m1 * rx1)
+                        cc = core if ry1 + rx1 else (c if core == 0 else 1 - c)
+                        hour = hours[zz * 32 + (yy // 2) * 16 + cc * 8 + (yy % 2) * 4 + xx]
+                        weights.append([jnp.where(hour - first == k, 1.0, 0.0).astype(jnp.float32) for k in range(slots)])
+            return weights
+
+        if ch not in EARLY_Z:
+            fixed = weights_of(z)
 
         @pl.loop(0, 4)
         def _(zt):
+            weights = weights_of((z - zt + 4) % 4) if ch in EARLY_Z else fixed
             for part_q in (0, 2):
                 pair = pl.ds(part_q, 2)
                 total = [None] * slots
@@ -137,22 +152,50 @@
                         for core in range(2):
                             if ry1 + rx1:
                                 raw = got1[ch, ry1, rx1, core, zt, pair]
-                            elif core == 0:
+                            elif core == 1:
+                                raw = got1[ch, 0, 0, 1 - c, zt, pair]
+                            elif ch in EARLY_Z:
+                                raw = raw_z[ch][zt, 0, 0, pair, c]
+                            else:
                                 raw = src[ch, 0, 0, zt, pair, c]
-                            else:
-                                raw = got1[ch, 0, 0, 1 - c, zt, pair]
                             value = rain_depth(raw)
                             for k in range(slots):
                                 term = value * weights[n][k]
                                 total[k] = term if total[k] is None else total[k] + term
                             n += 1
                 for k in range(slots):
-                    slots_of[ch][zt, k, pair] = total[k]
+                    if ch in EARLY_Z:
+                        gotz[ch][zt, LOW + k, pair] = total[k]
+                    elif ch in LATE_Z:
+                        slots_of[ch][pair, k, zt] = total[k]
+                    else:
+                        slots_of[ch][zt, k, pair] = total[k]
+
+    def copyr(ch, dz):
+        target_z = (z + dz) % 4
+        return pltpu.make_async_remote_copy(
+            src_ref=src.at[ch, :, :, target_z],
+            dst_ref=raw_z[ch].at[dz],
+            send_sem=sendr.at[ch, dz],
+            recv_sem=recvr.at[ch, dz],
+            device_id=device(x, y, target_z, c),
+            device_id_type=MESH,
+        )
+
+    def copyr_own(ch):
+        return pltpu.make_async_copy(src.at[ch, :, :, z], raw_z[ch].at[0], localr.at[ch])
+
+    def startz(ch, steps=(2, 1, 3)):
+        for dz in steps:
+            copyr(ch, dz).start()
+        if 1 in steps:
+            copyr_own(ch).start()
 
     def copyz(ch, dz):
         target_z = (z + dz) % 4
-        return pltpu.make_async_remote_copy(
-            src_ref=slots_of[ch].at[target_z],
+        block = sumz[ch] if ch in LATE_Z else slots_of[ch]
+        return pltpu.make_async_remote_copy(
+            src_ref=block.at[target_z],
             dst_ref=gotz[ch].at[dz, pl.ds(LOW, SLOTS[ch % 2])],
             send_sem=sendz.at[ch, dz],
             recv_sem=recvz.at[ch, dz],
@@ -168,8 +211,9 @@
 
     def copyq(ch, q):
         _, m2 = masks(ch % 2)
-        return pltpu.make_async_remote_copy(
-            src_ref=sumz[ch].at[q],
+        block = slots_of[ch] if ch in LATE_Z else sumz[ch]
+        return pltpu.make_async_remote_copy(
+            src_ref=block.at[q],
             dst_ref=gotq[ch].at[q - 1],
             send_sem=sendq.at[ch, q],
             recv_sem=recvq.at[ch, q],
@@ -181,38 +225,72 @@
         for ch in which:
             pltpu.make_async_copy(src.at[ch], src.at[ch], load_sem.at[ch]).wait()
 
-    def start1(pair):
-        for one, two in zip(step1_copies(2 * pair, True), step1_copies(2 * pair + 1, True)):
+    def start1(pair, which=slice(0, 7)):
+        for ch in (2 * pair, 2 * pair + 1):
+            if ch in EARLY_Z:
+                copyr_own(ch).wait()
+                for dz in (1, 2, 3):
+                    copyr(ch, dz).wait_recv()
+        for one, two in zip(step1_copies(2 * pair, True, which), step1_copies(2 * pair + 1, True, which)):
             one.start()
             two.start()
 
-    def first(pair):
-        for ch in (2 * pair, 2 * pair + 1):
+    def send_z(ch, block):
+        for dz in (2, 1, 3):
+            copyz(ch, dz).start()
+        for k in range(SLOTS[ch % 2]):
+            gotz[ch][0, LOW + k] = block[z, k]
+
+    def send_q(ch):
+        for q in (3, 1, 2):
+            copyq(ch, q).start()
+
+    def first(*which):
+        for ch in which:
             for copy in step1_copies(ch, False):
                 copy.wait_recv()
             reduce1(ch)
-            for dz in (2, 1, 3):
-                copyz(ch, dz).start()
-            for k in range(SLOTS[ch % 2]):
-                gotz[ch][0, LOW + k] = slots_of[ch][z, k]
-
-    def second(pair):
-        for ch in (2 * pair, 2 * pair + 1):
-            for dz in (1, 2, 3):
-                copyz(ch, dz).wait_recv()
-            combinez(ch)
-            for q in (3, 1, 2):
-                copyq(ch, q).start()
-
-    def third(pair):
-        for ch in (2 * pair, 2 * pair + 1):
-            for q in (1, 2, 3):
-                copyq(ch, q).wait_recv()
-            j, half = ch // 2, ch % 2
+            if ch in EARLY_Z:
+                combinez(ch)
+            if ch in EARLY_Z + LATE_Z:
+                send_q(ch)
+            else:
+                send_z(ch, slots_of[ch])
+
+    def second(*which):
+        for ch in which:
+            if ch in LATE_Z:
+                for q in (1, 2, 3):
+                    copyq(ch, q).wait_recv()
+                for zt in range(4):
+                    for k in range(SLOTS[ch % 2]):
+                        sumz[ch][zt, k] = (slots_of[ch][0, k, zt] + gotq[ch][0, k, zt]) + (
+                            gotq[ch][1, k, zt] + gotq[ch][2, k, zt]
+                        )
+                send_z(ch, sumz[ch])
+            else:
+                for dz in (1, 2, 3):
+                    copyz(ch, dz).wait_recv()
+                combinez(ch)
+                send_q(ch)
+
+    def third(*which):
+        for ch in which:
+            band = slice(ch // 2 * 8, ch // 2 * 8 + 8)
+            half = slice(ch % 2 * 128, ch % 2 * 128 + 128)
+            if ch in LATE_Z:
+                for dz in (1, 2, 3):
+                    copyz(ch, dz).wait_recv()
+                starts = [LOW - hours[base_scan(ch, (z - dz + 4) % 4)] for dz in range(4)]
+            else:
+                for q in (1, 2, 3):
+                    copyq(ch, q).wait_recv()
             for h in range(HOURS):
-                out[h, j * 8 : (j + 1) * 8, half * 128 : (half + 1) * 128] = (
-                    (sumz[ch][0, h] + gotq[ch][0, h]) + (gotq[ch][1, h] + gotq[ch][2, h])
-                )
+                if ch in LATE_Z:
+                    terms = [gotz[ch][dz, starts[dz] + h] for dz in range(4)]
+                else:
+                    terms = [sumz[ch][0, h]] + [gotq[ch][n, h] for n in range(3)]
+                out[h, band, half] = (terms[0] + terms[1]) + (terms[2] + terms[3])
 
     lane = lax.broadcasted_iota(jnp.int32, (8, 128), 1)
 
@@ -250,7 +328,7 @@
 
     def ecopy2(dz):
         return pltpu.make_async_remote_copy(
-            src_ref=seg_hours,
+            src_ref=seg_hours.at[dz],
             dst_ref=got_hours.at[dz - 1],
             send_sem=esend2.at[dz],
             recv_sem=erecv2.at[dz],
@@ -277,7 +355,7 @@
         return found + [copy(0, 0, c, 1 - c)]
 
     def segments1():
-        loaded(*range(2, CHUNKS))
+        loaded(*[ch for ch in range(2, CHUNKS) if ch not in EARLY_Z])
         own_segments()
         for copy in quad_out(ecopy1):
             copy.start()
@@ -300,8 +378,15 @@
                     for h in range(HOURS):
                         term = value * jnp.where(hour == h, 1.0, 0.0).astype(jnp.float32)
                         totals[h] = term if totals[h] is None else totals[h] + term
-        for h in range(HOURS):
-            seg_hours[h] = totals[h]
+        for dz in (2, 1, 3, 0):
+            for k in range(HOURS // 4):
+                packed = jnp.zeros((8, 128), jnp.float32)
+                for h in range(4 * k, 4 * k + 4):
+                    value = jnp.where(lane // 32 == (z + dz) % 4, totals[h], 0.0)
+                    value = value + pltpu.roll(value, 64, 1)
+                    value = value + pltpu.roll(value, 32, 1)
+                    packed = jnp.where(lane // 32 == h % 4, value, packed)
+                seg_hours[dz, k] = packed
         for dz in (2, 1, 3):
             ecopy2(dz).start()
 
@@ -309,14 +394,7 @@
         for dz in (1, 2, 3):
             ecopy2(dz).wait_recv()
         for k in range(HOURS // 4):
-            packed = jnp.zeros((8, 128), jnp.float32)
-            for h in range(4 * k, 4 * k + 4):
-                value = (seg_hours[h] + got_hours[0, h]) + (got_hours[1, h] + got_hours[2, h])
-                value = jnp.where(lane // 32 == z, value, 0.0)
-                value = value + pltpu.roll(value, 64, 1)
-                value = value + pltpu.roll(value, 32, 1)
-                packed = jnp.where(lane // 32 == h % 4, value, packed)
-            seg_pack[k] = packed
+            seg_pack[k] = (seg_hours[0, k] + got_hours[0, k]) + (got_hours[1, k] + got_hours[2, k])
         for q in (3, 1, 2):
             ecopy3(q).start()
 
@@ -431,35 +509,54 @@
         )
 
     loaded(0, 1)
-    start1(0)
+    start1(0, slice(0, 5))
+    for ch in range(2, CHUNKS):
+        if ch not in EARLY_Z:
+            load(ch)
+    loaded(*EARLY_Z)
+    startz(6)
+    startz(7, (2,))
     segments1()
+    start1(0, slice(5, 7))
     start1(1)
+    clear()
+    segments2()
+    startz(7, (1, 3))
     first(0)
-    segments2()
-    start1(2)
     first(1)
     segments3()
+    start1(2)
+    shares()
     start1(3)
+    first(3)
+    first(2)
     second(0)
-    first(2)
-    shares()
+    shares2()
+    first(4)
     second(1)
+    first(5)
+    second(2)
+    second(4)
+    first(7)
+    first(6)
     third(0)
-    first(3)
-    shares2()
-    second(2)
-    third(1)
     shares3()
     second(3)
+    second(5)
     third(2)
     shares4()
+    third(1)
+    third(4)
     third(3)
+    third(7)
+    third(6)
+    third(5)
 
     for ch in range(CHUNKS):
         for copy in step1_copies(ch, True):
             copy.wait_send()
         for dz in (1, 2, 3):
-            copyz(ch, dz).wait_send()
+            (copyr if ch in EARLY_Z else copyz)(ch, dz).wait_send()
         for q in (1, 2, 3):
             copyq(ch, q).wait_send()
     for copy in quad_out(ecopy1) + quad_out(bcopy1):
@@ -485,15 +582,17 @@
     scratch = [
         vmem(CHUNKS, 2, 2, 4, 4, 2, 8, 128),
         vmem(CHUNKS, 2, 2, 2, 4, 4, 8, 128),
-        *[vmem(4, SLOTS[ch % 2], 4, 8, 128) for ch in chunks],
-        *[vmem(4, HOURS + LOW, 4, 8, 128) for ch in chunks],
-        *[vmem(4, HOURS, 8, 128) for ch in chunks],
-        *[vmem(3, HOURS, 8, 128) for ch in chunks],
-        vmem(2, 2, 2, 8, 128), vmem(2, 2, 2, 8, 128), vmem(HOURS, 8, 128), vmem(3, HOURS, 8, 128),
+        *[vmem(4, 1 if ch in EARLY_Z else SLOTS[ch % 2], 4, 8, 128) for ch in chunks],
+        *[vmem(4, HOURS + LOW, *((8, 128) if ch in LATE_Z else (4, 8, 128))) for ch in chunks],
+        *[vmem(4, SLOTS[1] if ch in LATE_Z else HOURS, 8, 128) for ch in chunks],
+        *[vmem(3, *((SLOTS[1], 4) if ch in LATE_Z else (HOURS,)), 8, 128) for ch in chunks],
+        vmem(2, 2, 2, 8, 128), vmem(2, 2, 2, 8, 128), vmem(4, HOURS // 4, 8, 128), vmem(3, HOURS // 4, 8, 128),
         vmem(HOURS // 4, 8, 128), vmem(3, HOURS // 4, 8, 128),
         vmem(8, 16, 128), vmem(8, 16, 128), vmem(16, 128), vmem(3, 16, 128), vmem(8, 128), vmem(3, 8, 128),
         dma(CHUNKS), dma(CHUNKS, 8), dma(CHUNKS, 8), dma(CHUNKS, 4), dma(CHUNKS, 4), dma(CHUNKS, 4), dma(CHUNKS, 4),
         dma(8), dma(8), dma(4), dma(4), dma(4), dma(4), dma(8), dma(8), dma(4), dma(4), dma(4), dma(4),
+        *[vmem(4, 2, 2, 4, 2, 8, 128) for ch in EARLY_Z],
+        dma(CHUNKS, 4), dma(CHUNKS, 4), dma(CHUNKS),
     ]
     block = pl.BlockSpec(memory_space=pltpu.VMEM)
     hourly, table = pl.pallas_call(

time: 57.6 us -> 50.4 us (0.88); the launches traced: 57.4 us -> 49.6 us
  Pallas kernels: 55.5 us -> 47.6 us
    pallas_call x1, Pallas kernels: 54.7 us -> 46.8 us  [body(): pl.pallas_call(kernel, out_shape=(jax.ShapeDtypeStruct((HOURS, 32, 256),...]
where the time goes in v4:
time: 50.4 us; the launch traced here: 49.6 us
  Pallas kernels  47.6 us (94%)
  local copies, waits for them, and re-layouts  1.33 us (3%)
  between operations  0.65 us (1%)
    pallas_call x1, Pallas kernels, body(): pl.pallas_call(kernel, out_shape=(jax.ShapeDtypeStruct((HOURS, 32, 256),...  46.8 us
    unnamed x4, local copies, waits for them, and re-layouts  1.33 us

profile of v4, /device:TPU:1, one launch (start us, length us, event | category | flops | bytes accessed | tf_op | source)
XLA Modules:
  0.0 49.6 jit_solution(15326957532075477942)
XLA Ops:
  0.6 0.0 copy-start
  0.6 0.7 %copy-done = s32[32,2]{0,1:T(2,128)S(1)} copy-done((s32[32,2]{0,1:T(2,128)S(1)}, s32[32,2]{0,1:T(2,128)}, u32[]{:S(2)}) %copy-start) | copy-done | bytes 280
  1.3 0.0 copy-start.1
  1.3 0.7 %copy-done.1 = s32[128]{0:T(128)S(1)} copy-done((s32[128]{0:T(128)S(1)}, s32[128]{0:T(128)}, u32[]{:S(2)}) %copy-start.1) | copy-done | bytes 536
  2.0 46.8 %shard_map.50 = (f32[12,32,256]{2,1,0:T(8,128)S(1)}, f32[8,128]{1,0:T(8,128)S(1)}) custom-call(f32[4,2,2,4,8,2048]{5,4,3,2,1,0:T(8,128)} %bitcast.3, s32[128]{0:T(128)S(1)} %copy-done.1, s32[2,32]{1,0:T(2,128)S(1)} %bitcast.2), custom_call_target="tpu_custom_call" | custom-call | tf_op jit(solution)/shard_map/pallas_call | solution.py:598
  48.8 0.8 %shard_map.51 = (f32[12,32,256]{2,1,0:T(8,128)}, f32[8,12]{1,0:T(8,128)}) custom-call(f32[12,32,256]{2,1,0:T(8,128)S(1)} %get-tuple-element.4.hourly, f32[8,128]{1,0:T(8,128)S(1)} %get-tuple-element.5.table), custom_call_target="tpu_custom_call" | custom-call | tf_op jit(solution)/shard_map/pallas_call | solution.py:611
Async XLA Ops:
  0.6 0.7 %copy-start = (s32[32,2]{0,1:T(2,128)S(1)}, s32[32,2]{0,1:T(2,128)}, u32[]{:S(2)}) copy-start(s32[32,2]{0,1:T(2,128)} %param.5) | copy-start | bytes 772
  1.3 0.7 %copy-start.1 = (s32[128]{0:T(128)S(1)}, s32[128]{0:T(128)}, u32[]{:S(2)}) copy-start(s32[128]{0:T(128)} %hours.1) | copy-start | bytes 1540

commit v5 on v4

--- a/solution.py
+++ b/solution.py
@@ -43,16 +43,16 @@
     return (z * 4 + (y // 2) * 2 + c, (y % 2) * 4 + x)
 
 
-def kernel(refl, hours, ids, out, table_out, *scratch):
+def kernel(refl, hours_in, ids_in, out, table_out, *scratch):
     src, got1 = scratch[:2]
     slots_of, gotz, sumz, gotq = (scratch[2 + CHUNKS * i : 2 + CHUNKS * (i + 1)] for i in range(4))
     (
         own_seg, got_seg, seg_hours, got_hours, seg_pack, got_pack, part, part_got, part_sum, part_last, row_sum, row_got,
         load_sem, send1, recv1, sendz, recvz, sendq, recvq, esend1, erecv1, esend2, erecv2, esend3, erecv3,
         bsend1, brecv1, bsend2, brecv2, bsend3, brecv3,
-    ) = scratch[2 + CHUNKS * 4 : len(scratch) - 3 - len(EARLY_Z)]
-    raw_z = dict(zip(EARLY_Z, scratch[len(scratch) - 3 - len(EARLY_Z) :]))
-    sendr, recvr, localr = scratch[-3:]
+    ) = scratch[2 + CHUNKS * 4 : len(scratch) - 6 - len(EARLY_Z)]
+    raw_z = dict(zip(EARLY_Z, scratch[len(scratch) - 6 - len(EARLY_Z) :]))
+    sendr, recvr, localr, hours, ids, table_sem = scratch[-6:]
     row, col = lax.axis_index("row"), lax.axis_index("col")
     z, c = row // 4, row % 2
     y, x = ((row // 2) % 2) * 2 + col // 4, col % 4
@@ -68,6 +68,11 @@
         peers.append(device(x, y, (z + dz) % 4, c))
     for peer in peers:
         pl.semaphore_signal(barrier, inc=1, device_id=peer, device_id_type=MESH)
+
+    fetches = [
+        pltpu.make_async_copy(hours_in, hours, table_sem.at[0]),
+        pltpu.make_async_copy(ids_in, ids, table_sem.at[1]),
+    ]
 
     def load(ch):
         m1, m2 = masks(ch % 2)
@@ -85,6 +90,8 @@
 
     for ch in (0, 1) + EARLY_Z:
         load(ch)
+    for copy in fetches:
+        copy.start()
     pl.semaphore_wait(barrier, len(peers))
 
     def clear():
@@ -508,6 +515,18 @@
             spread, pick, precision=lax.Precision.HIGHEST, preferred_element_type=jnp.float32
         )
 
+    def sent():
+        for ch in range(CHUNKS):
+            for copy in step1_copies(ch, True):
+                copy.wait_send()
+            for dz in (1, 2, 3):
+                (copyr if ch in EARLY_Z else copyz)(ch, dz).wait_send()
+        for copy in quad_out(ecopy1) + quad_out(bcopy1):
+            copy.wait_send()
+        for n in (1, 2, 3):
+            for small in (ecopy2, ecopy3, bcopy2, bcopy3):
+                small(n).wait_send()
+
     loaded(0, 1)
     start1(0, slice(0, 5))
     for ch in range(2, CHUNKS):
@@ -517,6 +536,8 @@
     startz(6)
     startz(7, (2,))
     segments1()
+    for copy in fetches:
+        copy.wait()
     start1(0, slice(5, 7))
     start1(1)
     clear()
@@ -547,23 +568,15 @@
     shares4()
     third(1)
     third(4)
+    sent()
     third(3)
     third(7)
     third(6)
     third(5)
 
     for ch in range(CHUNKS):
-        for copy in step1_copies(ch, True):
-            copy.wait_send()
-        for dz in (1, 2, 3):
-            (copyr if ch in EARLY_Z else copyz)(ch, dz).wait_send()
         for q in (1, 2, 3):
             copyq(ch, q).wait_send()
-    for copy in quad_out(ecopy1) + quad_out(bcopy1):
-        copy.wait_send()
-    for n in (1, 2, 3):
-        for small in (ecopy2, ecopy3, bcopy2, bcopy3):
-            small(n).wait_send()
 
 
 def finish(hourly, table, out, depth):
@@ -593,6 +606,7 @@
         dma(8), dma(8), dma(4), dma(4), dma(4), dma(4), dma(8), dma(8), dma(4), dma(4), dma(4), dma(4),
         *[vmem(4, 2, 2, 4, 2, 8, 128) for ch in EARLY_Z],
         dma(CHUNKS, 4), dma(CHUNKS, 4), dma(CHUNKS),
+        pltpu.SMEM((128,), jnp.int32), pltpu.VMEM((2, 32), jnp.int32), dma(2),
     ]
     block = pl.BlockSpec(memory_space=pltpu.VMEM)
     hourly, table = pl.pallas_call(
@@ -601,7 +615,7 @@
             jax.ShapeDtypeStruct((HOURS, 32, 256), jnp.float32),
             jax.ShapeDtypeStruct((8, 128), jnp.float32),
         ),
-        in_specs=[pl.BlockSpec(memory_space=pl.ANY), pl.BlockSpec(memory_space=pltpu.SMEM), block],
+        in_specs=[pl.BlockSpec(memory_space=pl.ANY)] * 3,
         out_specs=(block, block),
         scratch_shapes=scratch,
         compiler_params=pltpu.CompilerParams(

time: 50.4 us -> 49.5 us (0.982)
  Pallas kernels: 47.6 us -> 46.8 us
    pallas_call x1, Pallas kernels: 46.8 us -> 46 us  [body(): pl.pallas_call(kernel, out_shape=(jax.ShapeDtypeStruct((HOURS, 32, 256),...]
where the time goes in v5:
time: 49.5 us; the launch traced here: 48.7 us
  Pallas kernels  46.8 us (95%)
  local copies, waits for them, and re-layouts  1.33 us (3%)
  between operations  0.65 us (1%)
    pallas_call x1, Pallas kernels, body(): pl.pallas_call(kernel, out_shape=(jax.ShapeDtypeStruct((HOURS, 32, 256),...  46 us
    unnamed x4, local copies, waits for them, and re-layouts  1.33 us

profile of v5, /device:TPU:1, one launch (start us, length us, event | category | flops | bytes accessed | tf_op | source)
XLA Modules:
  0.0 48.7 jit_solution(16790414539471684928)
XLA Ops:
  0.6 0.0 copy-start
  0.6 0.7 %copy-done = s32[32,2]{0,1:T(2,128)S(1)} copy-done((s32[32,2]{0,1:T(2,128)S(1)}, s32[32,2]{0,1:T(2,128)}, u32[]{:S(2)}) %copy-start) | copy-done | bytes 280
  1.3 0.0 copy-start.1
  1.3 0.7 %copy-done.1 = s32[128]{0:T(128)S(1)} copy-done((s32[128]{0:T(128)S(1)}, s32[128]{0:T(128)}, u32[]{:S(2)}) %copy-start.1) | copy-done | bytes 536
  2.0 46.0 %shard_map.50 = (f32[12,32,256]{2,1,0:T(8,128)S(1)}, f32[8,128]{1,0:T(8,128)S(1)}) custom-call(f32[4,2,2,4,8,2048]{5,4,3,2,1,0:T(8,128)} %bitcast.3, s32[128]{0:T(128)S(1)} %copy-done.1, s32[2,32]{1,0:T(2,128)S(1)} %bitcast.2), custom_call_target="tpu_custom_call" | custom-call | tf_op jit(solution)/shard_map/pallas_call | solution.py:612
  48.0 0.8 %shard_map.51 = (f32[12,32,256]{2,1,0:T(8,128)}, f32[8,12]{1,0:T(8,128)}) custom-call(f32[12,32,256]{2,1,0:T(8,128)S(1)} %get-tuple-element.4.hourly, f32[8,128]{1,0:T(8,128)S(1)} %get-tuple-element.5.table), custom_call_target="tpu_custom_call" | custom-call | tf_op jit(solution)/shard_map/pallas_call | solution.py:625
Async XLA Ops:
  0.6 0.7 %copy-start = (s32[32,2]{0,1:T(2,128)S(1)}, s32[32,2]{0,1:T(2,128)}, u32[]{:S(2)}) copy-start(s32[32,2]{0,1:T(2,128)} %param.5) | copy-start | bytes 772
  1.3 0.7 %copy-start.1 = (s32[128]{0:T(128)S(1)}, s32[128]{0:T(128)}, u32[]{:S(2)}) copy-start(s32[128]{0:T(128)} %hours_in.1) | copy-start | bytes 1540

commit v6 on v5

--- a/solution.py
+++ b/solution.py
@@ -243,7 +243,7 @@
             two.start()
 
     def send_z(ch, block):
-        for dz in (2, 1, 3):
+        for dz in (1, 3, 2):
             copyz(ch, dz).start()
         for k in range(SLOTS[ch % 2]):
             gotz[ch][0, LOW + k] = block[z, k]
@@ -528,7 +528,7 @@
                 small(n).wait_send()
 
     loaded(0, 1)
-    start1(0, slice(0, 5))
+    start1(0, slice(0, 4))
     for ch in range(2, CHUNKS):
         if ch not in EARLY_Z:
             load(ch)
@@ -538,7 +538,7 @@
     segments1()
     for copy in fetches:
         copy.wait()
-    start1(0, slice(5, 7))
+    start1(0, slice(4, 7))
     start1(1)
     clear()
     segments2()
@@ -552,10 +552,10 @@
     first(3)
     first(2)
     second(0)
+    first(4)
+    first(5)
     shares2()
-    first(4)
     second(1)
-    first(5)
     second(2)
     second(4)
     first(7)

time: 49.5 us -> 49.2 us (level)
  no operation moved by 1% of the time
where the time goes in v6:
time: 49.2 us; the launch traced here: 48.8 us
  Pallas kernels  46.9 us (95%)
  local copies, waits for them, and re-layouts  1.33 us (3%)
  between operations  0.65 us (1%)
    pallas_call x1, Pallas kernels, body(): pl.pallas_call(kernel, out_shape=(jax.ShapeDtypeStruct((HOURS, 32, 256),...  46.1 us
    unnamed x4, local copies, waits for them, and re-layouts  1.33 us

profile of v6, /device:TPU:1, one launch (start us, length us, event | category | flops | bytes accessed | tf_op | source)
XLA Modules:
  0.0 48.8 jit_solution(3833141583491272061)
XLA Ops:
  0.6 0.0 copy-start
  0.6 0.7 %copy-done = s32[32,2]{0,1:T(2,128)S(1)} copy-done((s32[32,2]{0,1:T(2,128)S(1)}, s32[32,2]{0,1:T(2,128)}, u32[]{:S(2)}) %copy-start) | copy-done | bytes 280
  1.3 0.0 copy-start.1
  1.3 0.7 %copy-done.1 = s32[128]{0:T(128)S(1)} copy-done((s32[128]{0:T(128)S(1)}, s32[128]{0:T(128)}, u32[]{:S(2)}) %copy-start.1) | copy-done | bytes 536
  2.0 46.1 %shard_map.50 = (f32[12,32,256]{2,1,0:T(8,128)S(1)}, f32[8,128]{1,0:T(8,128)S(1)}) custom-call(f32[4,2,2,4,8,2048]{5,4,3,2,1,0:T(8,128)} %bitcast.3, s32[128]{0:T(128)S(1)} %copy-done.1, s32[2,32]{1,0:T(2,128)S(1)} %bitcast.2), custom_call_target="tpu_custom_call" | custom-call | tf_op jit(solution)/shard_map/pallas_call | solution.py:612
  48.1 0.8 %shard_map.51 = (f32[12,32,256]{2,1,0:T(8,128)}, f32[8,12]{1,0:T(8,128)}) custom-call(f32[12,32,256]{2,1,0:T(8,128)S(1)} %get-tuple-element.4.hourly, f32[8,128]{1,0:T(8,128)S(1)} %get-tuple-element.5.table), custom_call_target="tpu_custom_call" | custom-call | tf_op jit(solution)/shard_map/pallas_call | solution.py:625
Async XLA Ops:
  0.6 0.7 %copy-start = (s32[32,2]{0,1:T(2,128)S(1)}, s32[32,2]{0,1:T(2,128)}, u32[]{:S(2)}) copy-start(s32[32,2]{0,1:T(2,128)} %param.5) | copy-start | bytes 772
  1.3 0.7 %copy-start.1 = (s32[128]{0:T(128)S(1)}, s32[128]{0:T(128)}, u32[]{:S(2)}) copy-start(s32[128]{0:T(128)} %hours_in.1) | copy-start | bytes 1540

commit v7 on v6

--- a/solution.py
+++ b/solution.py
@@ -544,17 +544,17 @@
     segments2()
     startz(7, (1, 3))
     first(0)
-    first(1)
     segments3()
     start1(2)
+    first(1)
     shares()
     start1(3)
     first(3)
     first(2)
-    second(0)
     first(4)
     first(5)
     shares2()
+    second(0)
     second(1)
     second(2)
     second(4)

time: 49.2 us -> 49.4 us (level)
  no operation moved by 1% of the time
where the time goes in v7:
time: 49.4 us; the launch traced here: 49.1 us
  Pallas kernels  47.1 us (95%)
  local copies, waits for them, and re-layouts  1.33 us (3%)
  between operations  0.65 us (1%)
    pallas_call x1, Pallas kernels, body(): pl.pallas_call(kernel, out_shape=(jax.ShapeDtypeStruct((HOURS, 32, 256),...  46.3 us
    unnamed x4, local copies, waits for them, and re-layouts  1.33 us

profile of v7, /device:TPU:1, one launch (start us, length us, event | category | flops | bytes accessed | tf_op | source)
XLA Modules:
  0.0 49.1 jit_solution(6818397867622468001)
XLA Ops:
  0.6 0.0 copy-start
  0.6 0.7 %copy-done = s32[32,2]{0,1:T(2,128)S(1)} copy-done((s32[32,2]{0,1:T(2,128)S(1)}, s32[32,2]{0,1:T(2,128)}, u32[]{:S(2)}) %copy-start) | copy-done | bytes 280
  1.3 0.0 copy-start.1
  1.3 0.7 %copy-done.1 = s32[128]{0:T(128)S(1)} copy-done((s32[128]{0:T(128)S(1)}, s32[128]{0:T(128)}, u32[]{:S(2)}) %copy-start.1) | copy-done | bytes 536
  2.0 46.3 %shard_map.50 = (f32[12,32,256]{2,1,0:T(8,128)S(1)}, f32[8,128]{1,0:T(8,128)S(1)}) custom-call(f32[4,2,2,4,8,2048]{5,4,3,2,1,0:T(8,128)} %bitcast.3, s32[128]{0:T(128)S(1)} %copy-done.1, s32[2,32]{1,0:T(2,128)S(1)} %bitcast.2), custom_call_target="tpu_custom_call" | custom-call | tf_op jit(solution)/shard_map/pallas_call | solution.py:612
  48.3 0.8 %shard_map.51 = (f32[12,32,256]{2,1,0:T(8,128)}, f32[8,12]{1,0:T(8,128)}) custom-call(f32[12,32,256]{2,1,0:T(8,128)S(1)} %get-tuple-element.4.hourly, f32[8,128]{1,0:T(8,128)S(1)} %get-tuple-element.5.table), custom_call_target="tpu_custom_call" | custom-call | tf_op jit(solution)/shard_map/pallas_call | solution.py:625
Async XLA Ops:
  0.6 0.7 %copy-start = (s32[32,2]{0,1:T(2,128)S(1)}, s32[32,2]{0,1:T(2,128)}, u32[]{:S(2)}) copy-start(s32[32,2]{0,1:T(2,128)} %param.5) | copy-start | bytes 772
  1.3 0.7 %copy-start.1 = (s32[128]{0:T(128)S(1)}, s32[128]{0:T(128)}, u32[]{:S(2)}) copy-start(s32[128]{0:T(128)} %hours_in.1) | copy-start | bytes 1540
